TPU v7x, 32 devices: a whole 2x2x4 slice. The times are simulated.
32 devices in a mesh: band: 8 (over z, x), img: 4 (over y, core).
Axes of the slice: x: 2, y: 2, z: 4, core: 2. Of those that a mesh axis runs over, the one named last changes fastest.
Arguments:
- pixels: bfloat16 [256, 256, 180], P(('img', 'band')), parts along dimension 0, may hold values from -12 to 12
- keep_mask: int32 [32, 32], P(('img', 'band')), parts along dimension 0, may hold values from 0 to 1, as said below
- band_counts: int32 [32], P(('img', 'band')), parts along dimension 0, may hold values from 0 to 32, as said below
- plan_dest: int32 [32, 16], P(('img', 'band')), parts along dimension 0, may hold values from 0 to 7, as said below
- plan_slot: int32 [32, 16], P(('img', 'band')), parts along dimension 0, may hold values from 0 to 8, as said below
- bias_table: float32 [225, 6], replicated, may hold values from -4 to 4
- gain_attn: float32 [180], replicated, may hold values from 0.25 to 1.75
- qkv_weight: bfloat16 [180, 540], replicated, may hold values from -5 to 5
- proj_weight: bfloat16 [180, 180], replicated, may hold values from -0.4375 to 0.4375
- gain_mlp: float32 [180], replicated, may hold values from 0.25 to 1.75
- hidden_weight: bfloat16 [180, 360], replicated, may hold values from -0.4375 to 0.4375
- output_weight: bfloat16 [360, 180], replicated, may hold values from -0.3125 to 0.3125
Outputs:
- restored: bfloat16 [256, 256, 180], P(('img', 'band')), parts along dimension 0
- work_tiles: bfloat16 [256, 128, 180], P(('img', 'band')), parts along dimension 0
There are 4 independent parts, one for each index of `img`. A program takes and returns all parts, laid end to end along the dimension named above; an argument that names none is the same for every part. Nothing has to cross between parts.
Inputs may be any that keep to these rules, and one draw needn't show every extreme that they name: `keep_mask`: the number of ones in a band varies strongly from band to band. band_counts[b] equals the number of ones among band b's windows in keep_mask. A band's live tiles are those with 2 t < band_counts[b]; their number summed over bands lies between 57 and 64, and some band has all 16 tiles live. `plan_dest`: within each aligned group of 8 consecutive tiles of a band (equal t // 8) the destinations are all different. `plan_slot`: 8 for tiles that are not live; a live tile has a slot below 8, no two live tiles of the image share destination and slot, and some destination receives 8 live tiles.
All inputs are finite; a program needn't handle non-finite values.
Results may differ from a plain program's by a relative error of at most 0.0044.
Values may be sent and summed in bfloat16 or wider, within the bound.
A program may use at most 64 MiB of HBM per device.

v0:
```python
import jax
import jax.numpy as jnp
from jax import lax
from jax.sharding import PartitionSpec as P

CHAN = 180
HEADS = 6
WIN = 8
TILE = 2
SHIFT = 4
CAP = 8


EPSILON = 1e-05


def from_behind(value, axis, steps):
    count = lax.axis_size(axis)
    pairs = [(source, (source + steps) % count) for source in range(count)]
    return lax.ppermute(value, axis, pairs)


def layer_norm(values, gain_vec):
    values = values.astype(jnp.float32)
    center = values - jnp.mean(values, axis=-1, keepdims=True)
    spread = jnp.mean(center * center, axis=-1, keepdims=True)
    return center * lax.rsqrt(spread + EPSILON) * gain_vec


def position_bias(bias_table):
    coords = jnp.arange(WIN * WIN, dtype=jnp.int32)
    row_pos = coords // WIN
    col_pos = coords % WIN
    table_index = (row_pos[:, None] - row_pos[None, :] + WIN - 1) * (2 * WIN - 1) + (
        col_pos[:, None] - col_pos[None, :] + WIN - 1
    )
    entries = bias_table.shape[0]
    onehot = (table_index.reshape(-1, 1) == jnp.arange(entries, dtype=jnp.int32)[None, :]).astype(
        jnp.float32
    )
    looked = jnp.dot(onehot, bias_table, precision=lax.Precision.HIGHEST)
    return jnp.transpose(looked.reshape(WIN * WIN, WIN * WIN, -1), (2, 0, 1))


def region_codes(first_row, row_count, height, col_count):
    rows_global = first_row + jnp.arange(row_count, dtype=jnp.int32)
    row_region = (rows_global >= height - WIN).astype(jnp.int32) + (
        rows_global >= height - SHIFT
    ).astype(jnp.int32)
    col_global = jnp.arange(col_count, dtype=jnp.int32)
    col_region = (col_global >= col_count - WIN).astype(jnp.int32) + (
        col_global >= col_count - SHIFT
    ).astype(jnp.int32)
    return 3 * row_region[:, None] + col_region[None, :]


def attend(windows, window_codes, head_bias, gain_attn, qkv_weight, proj_weight):
    window_count = windows.shape[0]
    head_dim = CHAN // HEADS
    normed = layer_norm(windows, gain_attn).astype(jnp.bfloat16).reshape(-1, CHAN)
    mixed_all = jnp.dot(normed, qkv_weight, preferred_element_type=jnp.float32).reshape(
        window_count, WIN * WIN, 3, HEADS, head_dim
    )
    queries = mixed_all[:, :, 0] * head_dim ** (-0.5)
    key_part = mixed_all[:, :, 1]
    value_part = mixed_all[:, :, 2].astype(jnp.bfloat16)
    scores = jnp.einsum("wqhd,wkhd->whqk", queries, key_part, precision=lax.Precision.HIGHEST)
    differ = window_codes[:, :, None] != window_codes[:, None, :]
    scores = scores + head_bias[None] + jnp.where(differ, -100.0, 0.0)[:, None]
    weights = jax.nn.softmax(scores, axis=-1).astype(jnp.bfloat16)
    mixed = jnp.einsum("whqk,wkhd->wqhd", weights, value_part, preferred_element_type=jnp.float32)
    mixed = mixed.reshape(-1, CHAN).astype(jnp.bfloat16)
    projected = jnp.dot(mixed, proj_weight, preferred_element_type=jnp.float32)
    summed = windows.reshape(-1, CHAN).astype(jnp.float32) + projected
    return summed.astype(jnp.bfloat16).reshape(window_count, WIN * WIN, CHAN)


def feed(states, gain_mlp, hidden_weight, output_weight):
    flat_rows = states.reshape(-1, CHAN)
    normed = layer_norm(flat_rows, gain_mlp).astype(jnp.bfloat16)
    inner_act = jax.nn.gelu(
        jnp.dot(normed, hidden_weight, preferred_element_type=jnp.float32)
    ).astype(jnp.bfloat16)
    summed = flat_rows.astype(jnp.float32) + jnp.dot(
        inner_act, output_weight, preferred_element_type=jnp.float32
    )
    return summed.astype(jnp.bfloat16).reshape(states.shape)


def shards(
    pixels,
    keep_mask,
    band_counts,
    plan_dest,
    plan_slot,
    bias_table,
    gain_attn,
    qkv_weight,
    proj_weight,
    gain_mlp,
    hidden_weight,
    output_weight,
):
    band_total = lax.axis_size("band")
    band_index = lax.axis_index("band")
    row_count, col_count, channels = pixels.shape
    win_rows = row_count // WIN
    win_cols = col_count // WIN
    window_total = win_rows * win_cols
    tile_total = window_total // TILE
    tile_tokens = TILE * WIN * WIN
    pair_slots = -(-tile_total // band_total)
    lower_rows = from_behind(pixels[:SHIFT], "band", -1)
    shifted = jnp.roll(jnp.concatenate([pixels[SHIFT:], lower_rows], axis=0), -SHIFT, axis=1)
    windows = (
        shifted.reshape(win_rows, WIN, win_cols, WIN, channels)
        .transpose(0, 2, 1, 3, 4)
        .reshape(window_total, WIN * WIN, channels)
    )
    region_map = region_codes(band_index * row_count, row_count, band_total * row_count, col_count)
    window_codes = (
        region_map.reshape(win_rows, WIN, win_cols, WIN)
        .transpose(0, 2, 1, 3)
        .reshape(window_total, WIN * WIN)
    )
    band_keep = keep_mask.reshape(window_total)
    kept_count = band_counts[0]
    packed_order = jnp.cumsum(band_keep) - 1
    active = (band_keep == 1) & (packed_order < kept_count)
    target = jnp.where(active, packed_order, window_total)
    packed = (
        jnp.zeros((window_total + 1, WIN * WIN, channels), jnp.bfloat16)
        .at[target]
        .set(windows)[:window_total]
    )
    packed_codes = (
        jnp.zeros((window_total + 1, WIN * WIN), jnp.bfloat16)
        .at[target]
        .set(window_codes.astype(jnp.bfloat16))[:window_total]
    )
    tile_ids = jnp.arange(tile_total, dtype=jnp.int32)
    tile_live = tile_ids * TILE < kept_count
    destinations = plan_dest[0]
    pair_index = tile_ids // band_total
    sent_slot = jnp.where(tile_live, plan_slot[0], CAP).astype(jnp.bfloat16)
    outgoing_slots = (
        jnp.full((band_total, pair_slots), CAP, jnp.bfloat16)
        .at[destinations, pair_index]
        .set(sent_slot)
    )
    head_bias = position_bias(bias_table)
    own_attended = attend(packed, packed_codes, head_bias, gain_attn, qkv_weight, proj_weight)
    flat_done = feed(own_attended, gain_mlp, hidden_weight, output_weight)
    outgoing = (
        jnp.zeros((band_total, pair_slots, tile_tokens, channels), jnp.bfloat16)
        .at[destinations, pair_index]
        .set(own_attended.reshape(tile_total, tile_tokens, channels))
    )
    incoming, incoming_slots = (
        lax.all_to_all(outgoing, "band", split_axis=0, concat_axis=0, tiled=True),
        lax.all_to_all(outgoing_slots, "band", split_axis=0, concat_axis=0, tiled=True),
    )
    arrived_slot = incoming_slots.reshape(-1).astype(jnp.int32)
    attended = (
        jnp.zeros((CAP, tile_tokens, channels), jnp.bfloat16)
        .at[arrived_slot]
        .set(incoming.reshape(-1, tile_tokens, channels), mode="drop")
    )
    gathered = flat_done[jnp.clip(packed_order, 0, window_total - 1)]
    result = jnp.where(active[:, None, None], gathered, windows)
    band_shifted = (
        result.reshape(win_rows, win_cols, WIN, WIN, channels)
        .transpose(0, 2, 1, 3, 4)
        .reshape(row_count, col_count, channels)
    )
    band_shifted = jnp.roll(band_shifted, SHIFT, axis=1)
    upper_rows = from_behind(band_shifted[row_count - SHIFT :], "band", 1)
    restored = jnp.concatenate([upper_rows, band_shifted[: row_count - SHIFT]], axis=0)
    return (restored, attended)


def solution(mesh):
    in_specs = (
        P(("img", "band"), None, None),
        P(("img", "band"), None),
        P(("img", "band")),
        P(("img", "band"), None),
        P(("img", "band"), None),
        P(),
        P(),
        P(),
        P(),
        P(),
        P(),
        P(),
    )
    out_specs = (P(("img", "band"), None, None), P(("img", "band"), None, None))
    return jax.shard_map(shards, mesh=mesh, in_specs=in_specs, out_specs=out_specs, check_vma=False)
```

profile of v0, /device:TPU:0, one launch (start us, length us, event | category | flops | bytes accessed | tf_op | source)
XLA Modules:
  0.0 99.3 jit_solution(17118073421504411057)
XLA Ops:
  0.7 1.7 %fusion.71 = (bf16[4,256,180]{1,0,2:T(4,128)(2,1)S(1)}, bf16[4,256,180]{1,0,2:T(4,128)(2,1)S(1)}) fusion(bf16[8,256,180]{1,0,2:T(8,128)(2,1)} %param.12), kind=kLoop, calls=%fused_computation.124 | loop fusion | bytes 1474560 | tf_op jit(solution)/shard_map/slice | solution.py:114
  2.7 6.1 %collective-permute-start = (bf16[4,256,180]{2,1,0:T(8,128)(2,1)S(1)}, bf16[4,256,180]{2,1,0:T(8,128)(2,1)S(1)}, u32[]{:S(2)}, u32[]{:S(2)}) collective-permute-start(bf16[4,256,180]{2,1,0:T(8,128)(2,1)S(1)} %copy.97), channel_id=1, source_target_pairs={{0,28},{4,0},{8,4},{12,8},{16,12},{20,16},{24,20},{28,24},{1,29},{... | collective-permute-start | bytes 1105928 | tf_op jit(solution)/shard_map/ppermute | solution.py:20
  9.5 1.3 %scatter_fusion.1 = bf16[8,2]{0,1:T(2,128)(2,1)S(1)} fusion(bf16[8,2]{0,1:T(2,128)(2,1)S(1)} %broadcast.478, s32[16]{0:T(128)S(1)} %fusion.64, bf16[16]{0:T(256)(128)(2,1)S(1)} %fusion.63), kind=kCustom, calls=%fused_computation.3 | custom fusion | bytes 224 | tf_op jit(solution)/shard_map/scatter | solution.py:149
  10.8 0.7 copy.88
  11.5 3.3 %all-to-all-start = ((bf16[8,1,2]{2,1,0:T(2,128)(2,1)}), bf16[8,1,2]{2,1,0:T(2,128)(2,1)S(1)}, u32[]{:S(2)}, u32[]{:S(2)}) async-start(bf16[8,1,2]{2,1,0:T(2,128)(2,1)} %copy.88), calls=%async_computation | async-start | bytes 8192 | tf_op jit(solution)/shard_map/all_to_all | solution.py:161
  15.3 2.6 %fusion.2 = f32[4096,6]{0,1:T(8,128)S(1)} fusion(f32[225,6]{0,1:T(8,128)S(1)} %copy-done.14, s32[4096]{0:T(1024)S(1)} %add.236), kind=kOutput, calls=%fused_computation.13 | convolution fusion | flops 67276800 | bytes 120088 | tf_op jit(solution)/shard_map/dot_general | solution.py:41
  18.5 0.8 reshape.414
  20.2 0.8 copy.81
  21.0 1.3 %compare_select_fusion = f32[32,64,64]{1,2,0:T(8,128)} fusion(bf16[32,64]{1,0:T(8,128)(2,1)S(1)} %slice.69), kind=kLoop, calls=%fused_computation.65 | loop fusion | flops 262144 | bytes 528384 | tf_op jit(solution)/shard_map/jit(_where)/select_n | solution.py:69
  23.5 1.8 %scatter_fusion = bf16[33,64,180]{2,1,0:T(8,128)(2,1)S(1)} fusion(bf16[33,64,180]{2,1,0:T(8,128)(2,1)S(1)} %broadcast_in_dim.26, s32[32]{0:T(128)S(1)} %get-tuple-element.13, bf16[32,64,180]{2,1,0:T(8,128)(2,1)S(1)} %copy_bitcast_fusion), kind=kCustom, calls=%fused_computation.1 | custom fusion | bytes 2211968 | tf_op jit(solution)/shard_map/scatter | solution.py:134
  25.6 1.6 %slice_convert_fusion.1 = f32[32,64,180]{2,1,0:T(8,128)} fusion(bf16[33,64,180]{2,1,0:T(8,128)(2,1)S(1)} %scatter_fusion), kind=kLoop, calls=%fused_computation.71 | loop fusion | flops 368640 | bytes 2211840 | tf_op jit(solution)/shard_map/convert_element_type | solution.py:74
  27.9 1.5 %fusion.33 = f32[32,64,3,6,30]{1,4,3,2,0:T(8,128)S(1)} fusion(bf16[3,6,30,180,1]{3,2,1,0,4:T(8,128)(2,1)S(1)} %copy-done.6, f32[180]{0:T(256)S(1)} %copy-done.11, f32[32,64]{1,0:T(8,128)S(1)} %add_rsqrt_fusion, f32[32,64]{1,0:T(8,128)S(1)} %broadcast_multiply_fusion, bf16[33,64,180]{2,1,0:T(8,128)(2,1)S(1)} %scatter_fusion), kind=kOutput, calls=%fused_computation.50 | convolution fusion | flops 399974400 | bytes 5800960 | tf_op jit(solution)/shard_map/dot_general | solution.py:61
  29.4 10.5 %fusion.3 = f32[32,6,64,64]{2,3,1,0:T(8,128)S(1)} fusion(f32[32,64,3,6,30]{1,4,3,2,0:T(8,128)S(1)} %fusion.33), kind=kOutput, calls=%fused_computation.15 | convolution fusion | flops 283484160 | bytes 9437184 | tf_op jit(solution)/shard_map/wqhd,wkhd->whqk/dot_general | solution.py:67
  39.9 3.7 %fusion.72 = (f32[32,6,64]{2,1,0:T(8,128)S(1)}, f32[32,6,64,64]{2,3,1,0:T(8,128)}) fusion(f32[32,6,64,64]{2,3,1,0:T(8,128)S(1)} %fusion.3, f32[32,64,64]{1,2,0:T(8,128)S(1)} %copy-done.7, f32[6,64,64]{1,2,0:T(8,128)S(1)} %bitcast.87), kind=kOutput, calls=%fused_computation.125 | output fusion | flops 4718655 | bytes 6963200 | tf_op jit(solution)/shard_map/sub | solution.py:70
  43.7 3.8 %fusion.29 = bf16[32,64,6,30]{1,3,2,0:T(8,128)(2,1)S(1)} fusion(f32[32,6,64,64]{2,3,1,0:T(8,128)} %get-tuple-element.17, f32[32,6,64]{2,1,0:T(8,128)S(1)} %get-tuple-element.16, f32[32,64,3,6,30]{1,4,3,2,0:T(8,128)S(1)} %fusion.33), kind=kOutput, calls=%fused_computation.48 | convolution fusion | flops 49127424 | bytes 5586944 | tf_op jit(solution)/shard_map/whqk,wkhd->wqhd/dot_general | solution.py:71
  47.5 2.1 %copy.84 = bf16[32,64,6,30]{1,0,3,2:T(8,128)(2,1)} copy(bf16[32,64,6,30]{1,3,2,0:T(8,128)(2,1)S(1)} %fusion.29) | data formatting | bytes 1474560 | tf_op jit(solution)/shard_map/convert_element_type | solution.py:72
  49.6 3.2 %convert_element_type.113 = bf16[2048,180]{0,1:T(8,128)(2,1)} reshape(bf16[32,64,6,30]{1,0,3,2:T(8,128)(2,1)} %copy.84) | data formatting | bytes 1474560 | tf_op jit(solution)/shard_map/convert_element_type | solution.py:72
  52.9 1.7 %copy.85 = f32[2048,180]{0,1:T(8,128)} copy(f32[2048,180]{1,0:T(8,128)S(1)} %bitcast.81) | data formatting | bytes 2949120 | tf_op jit(solution)/shard_map/convert_element_type | solution.py:74
  54.5 2.0 %convert_reduce_fusion = (f32[2048]{0:T(1024)S(1)}, bf16[2048,180]{0,1:T(8,128)(2,1)S(1)}) fusion(f32[2048,180]{0,1:T(8,128)} %copy.85, bf16[2048,180]{0,1:T(8,128)(2,1)} %convert_element_type.113, bf16[180,180]{1,0:T(8,128)(2,1)S(1)} %copy-done.10), kind=kOutput, calls=%fused_computation.35 | convolution fusion | flops 134182912 | bytes 3022112 | tf_op jit(solution)/shard_map/dot_general | solution.py:73
  57.4 1.6 %scatter_fusion.2 = bf16[8,2,128,180]{2,3,1,0:T(8,128)(2,1)S(1)} fusion(bf16[8,2,128,180]{2,3,1,0:T(8,128)(2,1)S(1)} %broadcast_in_dim.34, s32[16]{0:T(128)S(1)} %fusion.64, bf16[16,128,180]{1,2,0:T(8,128)(2,1)S(1)} %copy.89), kind=kCustom, calls=%fused_computation.4 | custom fusion | bytes 2211968 | tf_op jit(solution)/shard_map/scatter | solution.py:157
  59.1 1.5 %copy.90 = bf16[8,2,128,180]{2,1,3,0:T(2,128)(2,1)} copy(bf16[8,2,128,180]{2,3,1,0:T(8,128)(2,1)S(1)} %scatter_fusion.2) | data formatting | bytes 1474560 | tf_op jit(solution)/shard_map/scatter | solution.py:157
  60.6 6.0 %all-to-all-start.1 = ((bf16[8,2,128,180]{2,1,3,0:T(2,128)(2,1)}), bf16[8,2,128,180]{2,1,3,0:T(2,128)(2,1)}, u32[]{:S(2)}, u32[]{:S(2)}) async-start(bf16[8,2,128,180]{2,1,3,0:T(2,128)(2,1)} %copy.90), calls=%async_computation.1 | async-start | bytes 1474560 | tf_op jit(solution)/shard_map/all_to_all | solution.py:160
  66.5 2.4 %fusion.18 = bf16[2048,180]{0,1:T(8,128)(2,1)} fusion(bf16[360,180]{0,1:T(8,128)(2,1)S(1)} %copy-done, bf16[2048,180]{0,1:T(8,128)(2,1)S(1)} %get-tuple-element.19, bf16[180,360]{1,0:T(8,128)(2,1)S(1)} %copy-done.13, f32[180]{0:T(256)S(1)} %copy-done.15, f32[2048]{0:T(1024)S(1)} %add_rsqrt_fusion.1, f32[2048]{0:T(1024)S(1)} %broadcast_multiply_fusion.1), kind=kOutput, calls=%fused_computation.33 | convolution fusion | flops 540426240 | bytes 1750864 | tf_op jit(solution)/shard_map/dot_general | solution.py:84
  68.9 1.5 %copy.86 = bf16[2048,180]{1,0:T(8,128)(2,1)S(1)} copy(bf16[2048,180]{0,1:T(8,128)(2,1)} %fusion.18) | data formatting | bytes 1474560 | tf_op jit(solution)/shard_map/convert_element_type | solution.py:87
  70.5 1.6 %gather_fusion = bf16[32,64,180]{2,1,0:T(8,128)(2,1)} fusion(bf16[32,64,180]{2,1,0:T(8,128)(2,1)S(1)} %bitcast.84, s32[1024]{0:T(1024)S(1)} %pad_clamp_fusion), kind=kCustom, calls=%fused_computation | custom fusion | bytes 1474688 | tf_op jit(solution)/shard_map/gather | solution.py:169
  72.1 1.6 %fusion.38 = bf16[8,256,180]{2,1,0:T(8,128)(2,1)S(1)} fusion(pred[32]{0:T(512)(128)(4,1)S(1)} %bitcast_and_fusion, bf16[4,256,180]{2,1,0:T(8,128)(2,1)S(1)} %copy-done.5, bf16[4,256,180]{2,1,0:T(8,128)(2,1)S(1)} %copy-done.3, bf16[8,252,180]{2,1,0:T(8,128)(2,1)S(1)} %slice_maximum_fusion, bf16[32,64,180]{2,1,0:T(8,128)(2,1)} %gather_fusion), kind=kLoop, calls=%fused_computation.60 | loop fusion | flops 2580480 | bytes 2937632 | tf_op jit(solution)/shard_map/reshape | solution.py:174
  73.8 2.1 %collective-permute-start.1 = (bf16[4,256,180]{2,1,0:T(8,128)(2,1)S(1)}, bf16[4,256,180]{2,1,0:T(8,128)(2,1)S(1)}, u32[]{:S(2)}, u32[]{:S(2)}) collective-permute-start(bf16[4,256,180]{2,1,0:T(8,128)(2,1)S(1)} %fusion.51), channel_id=1, source_target_pairs={{0,4},{4,8},{8,12},{12,16},{16,20},{20,24},{24,28},{28,0},{1,5},{5... | collective-permute-start | bytes 1105928 | tf_op jit(solution)/shard_map/ppermute | solution.py:20
  76.0 18.2 %collective-permute-done.1 = bf16[4,256,180]{2,1,0:T(8,128)(2,1)S(1)} collective-permute-done((bf16[4,256,180]{2,1,0:T(8,128)(2,1)S(1)}, bf16[4,256,180]{2,1,0:T(8,128)(2,1)S(1)}, u32[]{:S(2)}, u32[]{:S(2)}) %collective-permute-start.1) | collective-permute-done | bytes 368672 | tf_op jit(solution)/shard_map/ppermute | solution.py:20
  94.4 1.4 %copy.92 = bf16[8,256,180]{1,0,2:T(8,128)(2,1)} copy(bf16[8,256,180]{2,1,0:T(8,128)(2,1)S(1)} %fusion.35) | data formatting | bytes 1474560
  95.8 1.2 %copy.91 = bf16[8,2,128,180]{2,3,1,0:T(8,128)(2,1)S(1)} copy(bf16[8,2,128,180]{2,1,3,0:T(2,128)(2,1)} %all-to-all-done.1) | data formatting | bytes 1474560 | tf_op jit(solution)/shard_map/all_to_all | solution.py:160
  97.0 1.4 %scatter_fusion.3 = bf16[8,128,180]{1,2,0:T(8,128)(2,1)S(1)} fusion(bf16[8,128,180]{1,2,0:T(8,128)(2,1)S(1)} %broadcast_in_dim.33, s32[16]{0:T(128)S(1)} %fusion.65, bf16[16,128,180]{1,2,0:T(8,128)(2,1)S(1)} %bitcast.83), kind=kCustom, calls=%fused_computation.5 | custom fusion | bytes 2211904 | tf_op jit(solution)/shard_map/scatter | solution.py:167
  98.5 0.8 copy.93
  (82 shorter events, 5.8 us)
Async XLA Ops:
  0.6 65.9 %copy-start = (bf16[360,180]{0,1:T(8,128)(2,1)S(1)}, bf16[360,180]{0,1:T(8,128)(2,1)}, u32[]{:S(2)}) copy-start(bf16[360,180]{0,1:T(8,128)(2,1)} %param.23) | copy-start | bytes 388804
  0.6 8.8 %copy-start.16 = (s32[1,16]{1,0:T(1,128)S(1)}, s32[1,16]{1,0:T(1,128)}, u32[]{:S(2)}) copy-start(s32[1,16]{1,0:T(1,128)} %param.15) | copy-start | bytes 196
  0.7 8.8 %copy-start.17 = (s32[1,16]{1,0:T(1,128)S(1)}, s32[1,16]{1,0:T(1,128)}, u32[]{:S(2)}) copy-start(s32[1,16]{1,0:T(1,128)} %param.16) | copy-start | bytes 196
  0.7 14.1 %copy-start.12 = (s32[1,32]{1,0:T(1,128)S(1)}, s32[1,32]{1,0:T(1,128)}, u32[]{:S(2)}) copy-start(s32[1,32]{1,0:T(1,128)} %param.13) | copy-start | bytes 388
  0.7 14.6 %copy-start.14 = (f32[225,6]{0,1:T(8,128)S(1)}, f32[225,6]{0,1:T(8,128)}, u32[]{:S(2)}) copy-start(f32[225,6]{0,1:T(8,128)} %param.17) | copy-start | bytes 16204
  2.4 16.0 %copy-start.8 = (bf16[180,540]{1,0:T(8,128)(2,1)S(1)}, bf16[180,540]{1,0:T(8,128)(2,1)}, u32[]{:S(2)}) copy-start(bf16[180,540]{1,0:T(8,128)(2,1)} %param.19) | copy-start | bytes 583204
  2.7 19.6 %collective-permute-start = (bf16[4,256,180]{2,1,0:T(8,128)(2,1)S(1)}, bf16[4,256,180]{2,1,0:T(8,128)(2,1)S(1)}, u32[]{:S(2)}, u32[]{:S(2)}) collective-permute-start(bf16[4,256,180]{2,1,0:T(8,128)(2,1)S(1)} %copy.97), channel_id=1, source_target_pairs={{0,28},{4,0},{8,4},{12,8},{16,12},{20,16},{24,20},{28,24},{1,29},{... | collective-permute-start | bytes 1105928 | tf_op jit(solution)/shard_map/ppermute | solution.py:20
  11.5 49.1 %all-to-all-start = ((bf16[8,1,2]{2,1,0:T(2,128)(2,1)}), bf16[8,1,2]{2,1,0:T(2,128)(2,1)S(1)}, u32[]{:S(2)}, u32[]{:S(2)}) async-start(bf16[8,1,2]{2,1,0:T(2,128)(2,1)} %copy.88), calls=%async_computation | async-start | bytes 8192 | tf_op jit(solution)/shard_map/all_to_all | solution.py:161
  18.3 4.3 %copy-start.2 = (bf16[4,256,180]{2,1,0:T(8,128)(2,1)}, bf16[4,256,180]{2,1,0:T(8,128)(2,1)S(1)}, u32[]{:S(2)}) copy-start(bf16[4,256,180]{2,1,0:T(8,128)(2,1)S(1)} %copy.96) | copy-start | bytes 1105924
  22.3 0.8 copy-start.4
  25.6 2.3 %copy-start.6 = (bf16[3,6,30,180,1]{3,2,1,0,4:T(8,128)(2,1)S(1)}, bf16[3,6,30,180,1]{3,2,1,0,4:T(8,128)(2,1)}, u32[]{:S(2)}) copy-start(bf16[3,6,30,180,1]{3,2,1,0,4:T(8,128)(2,1)} %reshape.414) | copy-start | bytes 583204
  25.6 2.3 %copy-start.11 = (f32[180]{0:T(256)S(1)}, f32[180]{0:T(256)}, u32[]{:S(2)}) copy-start(f32[180]{0:T(256)} %param.18) | copy-start | bytes 2164
  29.4 10.5 %copy-start.7 = (f32[32,64,64]{1,2,0:T(8,128)S(1)}, f32[32,64,64]{1,2,0:T(8,128)}, u32[]{:S(2)}) copy-start(f32[32,64,64]{1,2,0:T(8,128)} %compare_select_fusion) | copy-start | bytes 1572868
  29.4 10.5 %copy-start.9 = (f32[64,64,6]{0,1,2:T(8,128)S(1)}, f32[64,64,6]{0,1,2:T(8,128)}, u32[]{:S(2)}) copy-start(f32[64,64,6]{0,1,2:T(8,128)} %copy.81) | copy-start | bytes 294916
  47.5 5.3 %copy-start.1 = (f32[32,64,180]{2,1,0:T(8,128)S(1)}, f32[32,64,180]{2,1,0:T(8,128)}, u32[]{:S(2)}) copy-start(f32[32,64,180]{2,1,0:T(8,128)} %slice_convert_fusion.1) | copy-start | bytes 4423684
  52.8 1.7 %copy-start.10 = (bf16[180,180]{1,0:T(8,128)(2,1)S(1)}, bf16[180,180]{1,0:T(8,128)(2,1)}, u32[]{:S(2)}) copy-start(bf16[180,180]{1,0:T(8,128)(2,1)} %param.20) | copy-start | bytes 194404
  59.1 7.4 %copy-start.13 = (bf16[180,360]{1,0:T(8,128)(2,1)S(1)}, bf16[180,360]{1,0:T(8,128)(2,1)}, u32[]{:S(2)}) copy-start(bf16[180,360]{1,0:T(8,128)(2,1)} %param.22) | copy-start | bytes 388804
  59.1 7.4 %copy-start.15 = (f32[180]{0:T(256)S(1)}, f32[180]{0:T(256)}, u32[]{:S(2)}) copy-start(f32[180]{0:T(256)} %param.21) | copy-start | bytes 2164
  60.6 35.2 %all-to-all-start.1 = ((bf16[8,2,128,180]{2,1,3,0:T(2,128)(2,1)}), bf16[8,2,128,180]{2,1,3,0:T(2,128)(2,1)}, u32[]{:S(2)}, u32[]{:S(2)}) async-start(bf16[8,2,128,180]{2,1,3,0:T(2,128)(2,1)} %copy.90), calls=%async_computation.1 | async-start | bytes 1474560 | tf_op jit(solution)/shard_map/all_to_all | solution.py:160
  68.9 3.1 %copy-start.3 = (bf16[4,256,180]{2,1,0:T(8,128)(2,1)S(1)}, bf16[4,256,180]{2,1,0:T(8,128)(2,1)}, u32[]{:S(2)}) copy-start(bf16[4,256,180]{2,1,0:T(8,128)(2,1)} %copy-done.2) | copy-start | bytes 1105924
  68.9 3.1 %copy-start.5 = (bf16[4,256,180]{2,1,0:T(8,128)(2,1)S(1)}, bf16[4,256,180]{2,1,0:T(8,128)(2,1)}, u32[]{:S(2)}) copy-start(bf16[4,256,180]{2,1,0:T(8,128)(2,1)} %copy-done.4) | copy-start | bytes 1105924
  73.8 20.3 %collective-permute-start.1 = (bf16[4,256,180]{2,1,0:T(8,128)(2,1)S(1)}, bf16[4,256,180]{2,1,0:T(8,128)(2,1)S(1)}, u32[]{:S(2)}, u32[]{:S(2)}) collective-permute-start(bf16[4,256,180]{2,1,0:T(8,128)(2,1)S(1)} %fusion.51), channel_id=1, source_target_pairs={{0,4},{4,8},{8,12},{12,16},{16,20},{20,24},{24,28},{28,0},{1,5},{5... | collective-permute-start | bytes 1105928 | tf_op jit(solution)/shard_map/ppermute | solution.py:20
where the time goes:
time: 99.8 us; the launch traced here: 99.3 us
  local copies, waits for them, and re-layouts  28.2 us (28%)
  matrix products  22.8 us (23%)
  waiting for transfers between devices  18.2 us (18%)
  starting transfers between devices  17.4 us (17%)
  other arithmetic  10.9 us (11%)
  between operations  1.8 us (2%)
    ppermute x2, waiting for transfers between devices, from_behind(): return lax.ppermute(value, axis, pairs)  18.2 us
    dot_general x1, matrix products, attend(): jnp.einsum('wqhd,wkhd->whqk', queries, key_part, precision=lax.Precision....  10.5 us
    ppermute x2, starting transfers between devices, from_behind(): return lax.ppermute(value, axis, pairs)  8.13 us
    all_to_all x1, starting transfers between devices, shards(): lax.all_to_all(outgoing, 'band', split_axis=0, concat_axis=0, tiled=True)  5.95 us
    convert_element_type x2, local copies, waits for them, and re-layouts, attend(): mixed = mixed.reshape(-1, CHAN).astype(jnp.bfloat16)  5.31 us
    dot_general x1, matrix products, attend(): jnp.einsum('whqk,wkhd->wqhd', weights, value_part, preferred_element_type...  3.84 us
    sub x1, other arithmetic, attend(): weights = jax.nn.softmax(scores, axis=-1).astype(jnp.bfloat16)  3.74 us
    unnamed x41, local copies, waits for them, and re-layouts  3.47 us
  transfers between devices with their start and end apart: 4, of which 1 were waited for; matrix products, arithmetic and copies ran while one was open for 56% of the time, Pallas kernels for 0%

commit v1 on v0

v1 whole, which is shorter than its diff:
```python
import functools

import jax
import jax.numpy as jnp
from jax import lax
from jax.experimental import pallas as pl
from jax.experimental.pallas import tpu as pltpu
from jax.sharding import PartitionSpec as P

CHAN = 180
HEADS = 6
WIN = 8
TILE = 2
SHIFT = 4
CAP = 8
TOK = WIN * WIN
HALF = TOK // 2
HEAD_DIM = CHAN // HEADS
HEAD_PAD = 32
GROUP = 4

EPSILON = 1e-05
BF = jnp.bfloat16
F32 = jnp.float32


def layer_norm(values, gain_vec):
    center = values - jnp.sum(values, axis=-1, keepdims=True) * (1.0 / CHAN)
    spread = jnp.sum(center * center, axis=-1, keepdims=True) * (1.0 / CHAN)
    return (center * lax.rsqrt(spread + EPSILON) * gain_vec).astype(BF)


def dot(a, b):
    return jnp.dot(a, b, preferred_element_type=F32)


def dot_t(a, b):
    return lax.dot_general(a, b, (((1,), (1,)), ((), ())), preferred_element_type=F32)


def biases(bias_ref, last_row, queries):
    first = TOK - queries
    parts = [bias_ref[h][:, first:] for h in range(HEADS)]
    base = jnp.concatenate(parts, axis=1)
    shape = (TOK, HEADS * queries)
    key = lax.broadcasted_iota(jnp.int32, shape, 0)
    query = lax.broadcasted_iota(jnp.int32, shape, 1) % queries + first
    rows_differ = (key // WIN >= SHIFT) != (query // WIN >= SHIFT)
    cols_differ = (key % WIN >= SHIFT) != (query % WIN >= SHIFT)
    row_pen = jnp.where(rows_differ, jnp.where(last_row, -100.0, 0.0).astype(F32), 0.0)
    plain = base + row_pen
    both = base + jnp.where(cols_differ, -100.0, row_pen)
    return plain, both


def attend(x, gain, wq, wk, wvt, wp, masks, eye, bias_of, queries):
    normed = layer_norm(x, gain)
    if queries == TOK:
        x_q, n_q = x, normed
    else:
        pick = lambda a: jnp.concatenate(
            [a[g * TOK + TOK - queries : (g + 1) * TOK] for g in range(GROUP)], axis=0
        )
        x_q, n_q = pick(x), pick(normed)
    q = (dot(n_q, wq) * HEAD_DIM ** (-0.5)).astype(BF)
    k = dot(normed, wk).astype(BF)
    vt = dot_t(wvt, normed).astype(BF)
    mixed = []
    for g in range(GROUP):
        q_w = q[g * queries : (g + 1) * queries]
        stacked = jnp.concatenate([q_w * masks[h] for h in range(HEADS)], axis=0)
        scores = dot_t(k[g * TOK : (g + 1) * TOK], stacked) + bias_of(g)
        top = jnp.max(scores, axis=0, keepdims=True)
        grown = jnp.exp(scores - top)
        weights = (grown * (1.0 / jnp.sum(grown, axis=0, keepdims=True))).astype(BF)
        v_w = vt[:, g * TOK : (g + 1) * TOK]
        heads = [
            dot(
                v_w[h * HEAD_PAD : (h + 1) * HEAD_PAD],
                weights[:, h * queries : (h + 1) * queries],
            )
            for h in range(HEADS)
        ]
        mixed.append(jnp.concatenate(heads, axis=0))
    mixed = jnp.concatenate(mixed, axis=1).astype(BF)
    count = GROUP * queries
    mixed = dot_t(eye[:count, :count], mixed).astype(BF)
    return (x_q + dot(mixed, wp)).astype(BF)


def feed(states, gain, wh, wo):
    flat = states.astype(F32)
    normed = layer_norm(flat, gain)
    inner = jax.nn.gelu(dot(normed, wh)).astype(BF)
    return (flat + dot(inner, wo)).astype(BF)


def roll_cols(x, by):
    by = by % x.shape[1]
    return jnp.concatenate([x[:, by:], x[:, :by]], axis=1)


def block_kernel(
    keep_own, keep_prev, counts, dests,
    pixels, nxt, prv, bias, gain_a, wq_r, wk_r, wvt_r, wp_r, gain_m, wh_r, wo_r,
    restored, outgoing,
    shifted, result, attended, bias_own, bias_prev, act_own, act_prev, order,
):
    bands = lax.axis_size("band")
    me = lax.axis_index("band")
    cols = pixels.shape[1]
    windows = cols // WIN
    tiles = windows // TILE
    pairs = -(-tiles // bands)

    def scan(w, carry):
        own, prev = carry
        a = (keep_own[w] == 1) & (own < counts[0])
        b = (keep_prev[w] == 1) & (prev < counts[1])
        act_own[w] = a.astype(jnp.int32)
        act_prev[w] = b.astype(jnp.int32)
        order[own] = w
        return own + keep_own[w], prev + keep_prev[w]

    own_total, _ = lax.fori_loop(0, windows, scan, (jnp.int32(0), jnp.int32(0)))
    live = jnp.minimum(own_total, counts[0])

    shifted[0:SHIFT] = roll_cols(prv[...].astype(F32), SHIFT)
    shifted[SHIFT : SHIFT + WIN] = roll_cols(pixels[...].astype(F32), SHIFT)
    shifted[SHIFT + WIN :] = roll_cols(nxt[...].astype(F32), SHIFT)

    bias_own[0], bias_own[1] = biases(bias, me == bands - 1, TOK)
    bias_prev[0], bias_prev[1] = biases(bias, me == 0, HALF)

    lane = lax.broadcasted_iota(jnp.int32, (1, CHAN), 1)
    masks = [
        ((lane >= h * HEAD_DIM) & (lane < (h + 1) * HEAD_DIM)).astype(F32).astype(BF)
        for h in range(HEADS)
    ]
    side = GROUP * TOK
    eye = (
        lax.broadcasted_iota(jnp.int32, (side, side), 0)
        == lax.broadcasted_iota(jnp.int32, (side, side), 1)
    ).astype(F32).astype(BF)

    def step(i, _):
        def load(row, g):
            start = pl.multiple_of((i * GROUP + g) * WIN, WIN)
            return shifted[row : row + WIN, pl.ds(start, WIN), :].reshape(TOK, CHAN)

        def edge(ref):
            return lambda g: ref[(i * GROUP + g == windows - 1).astype(jnp.int32)]

        weights = (gain_a[...], wq_r[...], wk_r[...], wvt_r[...], wp_r[...])
        x_own = jnp.concatenate([load(WIN, g) for g in range(GROUP)], axis=0)
        own = attend(x_own, *weights, masks, eye, edge(bias_own), TOK)
        for g in range(GROUP):
            attended[i * GROUP + g] = own[g * TOK : (g + 1) * TOK]
        x_prev = jnp.concatenate([load(0, g) for g in range(GROUP)], axis=0)
        prev = attend(x_prev, *weights, masks, eye, edge(bias_prev), HALF)
        upper = jnp.concatenate([own[g * TOK : g * TOK + HALF] for g in range(GROUP)] + [prev], axis=0)
        done = feed(upper, gain_m[...], wh_r[...], wo_r[...]).astype(F32)
        for g in range(GROUP):
            w = i * GROUP + g
            start = pl.multiple_of(w * WIN, WIN)
            upper_new = done[g * HALF : (g + 1) * HALF].reshape(SHIFT, WIN, CHAN)
            lower_new = done[(GROUP + g) * HALF : (GROUP + g + 1) * HALF].reshape(SHIFT, WIN, CHAN)
            upper_old = x_own[g * TOK : g * TOK + HALF].reshape(SHIFT, WIN, CHAN)
            lower_old = x_prev[g * TOK + HALF : (g + 1) * TOK].reshape(SHIFT, WIN, CHAN)
            result[0:SHIFT, pl.ds(start, WIN), :] = jnp.where(act_prev[w] == 1, lower_new, lower_old)
            result[SHIFT:, pl.ds(start, WIN), :] = jnp.where(act_own[w] == 1, upper_new, upper_old)
        return 0

    lax.fori_loop(0, windows // GROUP, step, 0)
    restored[...] = roll_cols(result[...], -SHIFT).astype(BF)

    def pack(t, _):
        place = dests[t] * pairs + t // bands
        for p in range(TILE):
            position = t * TILE + p
            valid = position < live
            source = order[jnp.minimum(position, jnp.maximum(live - 1, 0))]
            source = jnp.where(valid, source, 0)
            value = attended[source]
            outgoing[place, p * TOK : (p + 1) * TOK] = jnp.where(valid, value, jnp.zeros_like(value))
        return 0

    lax.fori_loop(0, tiles, pack, 0)


def prepare(bias_table, qkv_weight, proj_weight):
    coords = jnp.arange(TOK, dtype=jnp.int32)
    row_pos, col_pos = coords // WIN, coords % WIN
    key, query = (slice(None), None), (None, slice(None))
    index = (row_pos[query] - row_pos[key] + WIN - 1) * (2 * WIN - 1) + (
        col_pos[query] - col_pos[key] + WIN - 1
    )
    entries = bias_table.shape[0]
    onehot = (jnp.arange(entries, dtype=jnp.int32)[:, None] == index.reshape(1, -1)).astype(F32)
    bias = jnp.dot(bias_table.T, onehot, precision=lax.Precision.HIGHEST).reshape(HEADS, TOK, TOK)
    pad = ((0, 0), (0, HEAD_PAD - HEAD_DIM), (0, 0))
    wvt = qkv_weight[:, 2 * CHAN :].T.reshape(HEADS, HEAD_DIM, CHAN)
    wvt = jnp.pad(wvt, pad).reshape(HEADS * HEAD_PAD, CHAN)
    wp = jnp.pad(proj_weight.reshape(HEADS, HEAD_DIM, CHAN), pad).reshape(HEADS * HEAD_PAD, CHAN)
    return bias, qkv_weight[:, :CHAN], qkv_weight[:, CHAN : 2 * CHAN], wvt, wp


def shards(
    pixels, keep_mask, band_counts, plan_dest, plan_slot, bias_table, gain_attn, qkv_weight,
    proj_weight, gain_mlp, hidden_weight, output_weight,
):
    bands = lax.axis_size("band")
    me = lax.axis_index("band")
    rows, cols, channels = pixels.shape
    windows = cols // WIN
    tiles = windows // TILE
    pairs = -(-tiles // bands)
    ahead = [(s, (s + 1) % bands) for s in range(bands)]
    back = [(s, (s - 1) % bands) for s in range(bands)]
    nxt = lax.ppermute(pixels[:SHIFT], "band", back)
    prv = lax.ppermute(pixels[rows - SHIFT :], "band", ahead)

    live_slot = jnp.where(
        jnp.arange(tiles, dtype=jnp.int32) * TILE < band_counts[0], plan_slot[0], CAP
    )
    facts = jnp.concatenate([keep_mask[0], band_counts, plan_dest[0], live_slot])
    facts = lax.all_gather(facts, "band", axis=0, tiled=False)
    before = lax.dynamic_index_in_dim(facts, (me - 1) % bands, 0, keepdims=False)
    keep_prev = before[:windows]
    counts = jnp.stack([band_counts[0], before[windows]])
    all_dest = facts[:, windows + 1 : windows + 1 + tiles]
    all_slot = facts[:, windows + 1 + tiles :]
    arrives = jnp.arange(bands, dtype=jnp.int32)[:, None] * pairs + (
        jnp.arange(tiles, dtype=jnp.int32) // bands
    )
    hit = (all_dest == me)[None] & (all_slot[None] == jnp.arange(CAP, dtype=jnp.int32)[:, None, None])
    source = jnp.max(jnp.where(hit, arrives[None], -1), axis=(1, 2))

    bias, wq, wk, wvt, wp = prepare(bias_table, qkv_weight, proj_weight)
    smem = pl.BlockSpec(memory_space=pltpu.SMEM)
    vmem = pl.BlockSpec(memory_space=pltpu.VMEM)
    restored, outgoing = pl.pallas_call(
        block_kernel,
        out_shape=(
            jax.ShapeDtypeStruct((rows, cols, channels), BF),
            jax.ShapeDtypeStruct((bands * pairs, TILE * TOK, channels), BF),
        ),
        in_specs=[smem] * 4 + [vmem] * 12,
        out_specs=(vmem, vmem),
        scratch_shapes=[
            pltpu.VMEM((rows + 2 * SHIFT, cols, channels), F32),
            pltpu.VMEM((rows, cols, channels), F32),
            pltpu.VMEM((windows, TOK, channels), BF),
            pltpu.VMEM((2, TOK, HEADS * TOK), F32),
            pltpu.VMEM((2, TOK, HEADS * HALF), F32),
            pltpu.SMEM((windows,), jnp.int32),
            pltpu.SMEM((windows,), jnp.int32),
            pltpu.SMEM((windows + 1,), jnp.int32),
        ],
        compiler_params=pltpu.CompilerParams(vmem_limit_bytes=60 * 1024 * 1024),
        name="block",
    )(
        keep_mask[0], keep_prev, counts, plan_dest[0],
        pixels, nxt, prv, bias, gain_attn[None], wq, wk, wvt, wp, gain_mlp[None],
        hidden_weight, output_weight,
    )
    incoming = lax.all_to_all(
        outgoing.reshape(bands, pairs, TILE * TOK, channels), "band", split_axis=0, concat_axis=0, tiled=True
    ).reshape(bands * pairs, TILE * TOK, channels)
    picked = jnp.take(incoming, jnp.maximum(source, 0), axis=0)
    work = jnp.where((source >= 0)[:, None, None], picked, jnp.zeros_like(picked))
    return restored, work


def solution(mesh):
    split = P(("img", "band"))
    in_specs = (split,) * 5 + (P(),) * 7
    return jax.shard_map(shards, mesh=mesh, in_specs=in_specs, out_specs=(split, split), check_vma=False)
```

time: 99.8 us -> 107 us (1.072)
  Pallas kernels: 0 us -> 35.1 us
  blocking collectives: 0 us -> 25.7 us
  matrix products: 22.8 us -> 1.3 us
  local copies, waits for them, and re-layouts: 28.2 us -> 15.3 us
  other arithmetic: 10.9 us -> 2.05 us
  starting transfers between devices: 17.4 us -> 9.68 us
  waiting for transfers between devices: 18.2 us -> 15.5 us
    pallas_call x0 -> x1, Pallas kernels: none -> 35.1 us  [shards(): pl.pallas_call(block_kernel, out_shape=(jax.ShapeDtypeStruct((rows, cols,...]
    unnamed x0 -> x1, blocking collectives: none -> 25.7 us
    dot_general x6 -> x1, matrix products: 22.8 us -> 1.3 us  [prepare(): jnp.dot(bias_table.T, onehot, precision=lax.Precision.HIGHEST)]
    ppermute x2, waiting for transfers between devices: 18.2 us -> 0.01 us  [the longest x1 0.01 us: shards(): nxt = lax.ppermute(pixels[:SHIFT], 'band', back)]
    all_to_all x2 -> x1, waiting for transfers between devices: 0.01 us -> 15.5 us  [shards(): lax.all_to_all(outgoing.reshape(bands, pairs, TILE * TOK, channels), 'ban...]
    convert_element_type x6 -> x0, local copies, waits for them, and re-layouts: 8.66 us -> none  [the longest x2 5.31 us: attend(): mixed = mixed.reshape(-1, CHAN).astype(jnp.bfloat16)]
    scatter x6 -> x0, local copies, waits for them, and re-layouts: 8.26 us -> none  [the longest x2 3.07 us: shards(): outgoing = jnp.zeros((band_total, pair_slots, tile_tokens, channels), jnp...]
    all_to_all x2 -> x1, starting transfers between devices: 9.23 us -> 3.68 us  [shards(): lax.all_to_all(outgoing.reshape(bands, pairs, TILE * TOK, channels), 'ban...]
  transfers between devices with their start and end apart: 4 -> 3, of which waited for: 1 -> 1; matrix products, arithmetic and copies ran while one was open for 56% -> 10% of each run, Pallas kernels for 0% -> 0%
where the time goes in v1:
time: 107 us
  Pallas kernels  35.1 us (33%)
  blocking collectives  25.7 us (24%)
  waiting for transfers between devices  15.5 us (14%)
  local copies, waits for them, and re-layouts  15.3 us (14%)
  starting transfers between devices  9.68 us (9%)
  between operations  2.18 us (2%)
  other arithmetic  2.05 us (2%)
  matrix products  1.3 us (1%)
    pallas_call x1, Pallas kernels, shards(): pl.pallas_call(block_kernel, out_shape=(jax.ShapeDtypeStruct((rows, cols,...  35.1 us
    unnamed x1, blocking collectives  25.7 us
    all_to_all x1, waiting for transfers between devices, shards(): lax.all_to_all(outgoing.reshape(bands, pairs, TILE * TOK, channels), 'ban...  15.5 us
    unnamed x30, local copies, waits for them, and re-layouts  6.94 us
    ppermute x1, starting transfers between devices, shards(): nxt = lax.ppermute(pixels[:SHIFT], 'band', back)  6 us
    all_to_all x1, starting transfers between devices, shards(): lax.all_to_all(outgoing.reshape(bands, pairs, TILE * TOK, channels), 'ban...  3.68 us
    reshape x1, local copies, waits for them, and re-layouts, shards(): outgoing.reshape(bands, pairs, TILE * TOK, channels)  3.16 us
  transfers between devices with their start and end apart: 3, of which 1 were waited for; matrix products, arithmetic and copies ran while one was open for 10% of the time, Pallas kernels for 0%

profile of v1, /device:TPU:0, one launch (start us, length us, event | category | flops | bytes accessed | tf_op | source)
XLA Modules:
  0.0 106.7 jit_solution(13717672814437218130)
XLA Ops:
  0.6 1.5 %copy.40.pixels = bf16[8,256,180]{2,1,0:T(8,128)(2,1)S(1)} copy(bf16[8,256,180]{1,0,2:T(8,128)(2,1)} %param.12) | data formatting | bytes 1474560 | tf_op args[0]
  2.3 0.8 copy-done.1
  3.2 6.0 %collective-permute-start = (bf16[4,256,180]{2,1,0:T(8,128)(2,1)S(1)}, bf16[4,256,180]{2,1,0:T(8,128)(2,1)S(1)}, u32[]{:S(2)}, u32[]{:S(2)}) collective-permute-start(bf16[4,256,180]{2,1,0:T(8,128)(2,1)S(1)} %get-tuple-element.15), channel_id=1, source_target_pairs={{0,28},{4,0},{8,4},{12,8},{16,12},{20,16},{24,20},{28,24},{1,29},{... | collective-permute-start | bytes 1105928 | tf_op jit(solution)/shard_map/ppermute | solution.py:220
  9.9 0.6 dynamic-slice
  11.1 0.2 add_dynamic-update-slice_fusion
  11.3 25.7 %all-reduce.2 = s32[520]{0:T(1024)S(1)} all-reduce(s32[520]{0:T(1024)S(1)} %add_dynamic-update-slice_fusion), channel_id=2, replica_groups=mesh['band'=8,'img'=4] {'band'}, use_global_device_ids=true, to_apply=%add.2 | all-reduce | flops 520 | bytes 4160
  37.0 0.1 reshape.190
  37.1 0.7 slice_bitcast_fusion
  37.8 0.1 add_add_fusion
  37.9 0.1 add.94
  38.0 1.3 %convolution_bitcast_fusion = f32[6,4096]{1,0:T(8,128)S(1)} fusion(f32[225,6]{0,1:T(8,128)S(1)} %copy-done, s32[4096]{0:T(1024)S(1)} %add.94), kind=kOutput, calls=%fused_computation.1 | convolution fusion | flops 67276800 | bytes 120088 | tf_op jit(solution)/shard_map/dot_general | solution.py:200
  39.4 0.6 slice.35
  40.0 0.1 copy.39
  40.1 0.8 reshape.175.bias
  40.9 0.6 pad.7
  41.6 0.6 pad.8
  42.2 0.8 copy.41.wo_r
  43.1 1.2 %pad_add_fusion.counts = s32[2]{0:T(128)} fusion(s32[1]{0:T(128)} %bitcast.6, s32[1]{0:T(128)} %copy.47), kind=kLoop, calls=%fused_computation.24 | loop fusion | flops 2 | bytes 16 | tf_op jit(solution)/shard_map/stack | solution.py:230
  44.3 0.6 slice_bitcast_fusion.1.keep_prev
  44.9 0.8 copy-done.3
  45.7 0.2 copy-done.4
  45.8 35.1 %block.1 = (bf16[8,256,180]{2,1,0:T(8,128)(2,1)}, bf16[16,128,180]{2,1,0:T(8,128)(2,1)}) custom-call(s32[32]{0:T(128)} %bitcast.25, s32[32]{0:T(128)} %slice_bitcast_fusion.1.keep_prev, s32[2]{0:T(128)} %pad_add_fusion.counts, s32[16]{0:T(128)} %bitcast.27, bf16[8,256,180]{2,1,0:T(8,128)(2,1)} %copy-done.1, bf16[4,256,180]{2,1,0:T(8,128)(2,1)} %copy-done.3, ...), custom_call_target="tpu_custom_call" | custom-call | tf_op jit(solution)/shard_map/block/pallas_call | solution.py:242
  80.9 3.2 %copy.42 = bf16[8,2,128,180]{2,1,3,0:T(2,128)(2,1)} copy(bf16[8,2,128,180]{3,2,1,0:T(8,128)(2,1)} %bitcast.22) | data formatting | bytes 1474560 | tf_op jit(solution)/shard_map/reshape | solution.py:268
  84.1 3.7 %all-to-all-start = ((bf16[8,2,128,180]{2,1,3,0:T(2,128)(2,1)}), bf16[8,2,128,180]{2,1,3,0:T(2,128)(2,1)S(1)}, u32[]{:S(2)}, u32[]{:S(2)}) async-start(bf16[8,2,128,180]{2,1,3,0:T(2,128)(2,1)} %copy.42), calls=%async_computation | async-start | bytes 1474560 | tf_op jit(solution)/shard_map/all_to_all | solution.py:267
  87.8 0.1 slice_compare_fusion
  87.9 0.2 select_reduce_fusion
  88.2 1.4 %copy.44 = bf16[8,256,180]{1,0,2:T(8,128)(2,1)} copy(bf16[8,256,180]{2,1,0:T(8,128)(2,1)S(1)} %copy-done.2) | data formatting | bytes 1474560
  89.6 15.5 %all-to-all-done = bf16[8,2,128,180]{2,1,3,0:T(2,128)(2,1)S(1)} async-done(((bf16[8,2,128,180]{2,1,3,0:T(2,128)(2,1)}), bf16[8,2,128,180]{2,1,3,0:T(2,128)(2,1)S(1)}, u32[]{:S(2)}, u32[]{:S(2)}) %all-to-all-start) | async-done | bytes 737312 | tf_op jit(solution)/shard_map/all_to_all | solution.py:267
  105.1 0.1 copy.43
  105.2 0.6 gather_fusion
  105.8 0.1 select_select_fusion
  106.0 0.8 copy.45
  (38 shorter events, 0.4 us)
Async XLA Ops:
  0.6 37.4 %copy-start = (f32[225,6]{0,1:T(8,128)S(1)}, f32[225,6]{0,1:T(8,128)}, u32[]{:S(2)}) copy-start(f32[225,6]{0,1:T(8,128)} %param.17) | copy-start | bytes 16204
  2.2 1.0 copy-start.1
  2.2 7.6 %copy-start.10 = (s32[1,16]{1,0:T(1,128)S(1)}, s32[1,16]{1,0:T(1,128)}, u32[]{:S(2)}) copy-start(s32[1,16]{1,0:T(1,128)} %param.16) | copy-start | bytes 196
  2.2 7.7 %copy-start.11 = (u32[32]{0:T(128)S(1)}, u32[32]{0:T(128)}, u32[]{:S(2)}) copy-start(u32[32]{0:T(128)} %constant.110) | copy-start | bytes 388
  2.2 8.9 %copy-start.8 = (s32[1,32]{1,0:T(1,128)S(1)}, s32[1,32]{1,0:T(1,128)}, u32[]{:S(2)}) copy-start(s32[1,32]{1,0:T(1,128)} %param.13) | copy-start | bytes 388
  2.2 8.9 %copy-start.9 = (s32[1,16]{1,0:T(1,128)S(1)}, s32[1,16]{1,0:T(1,128)}, u32[]{:S(2)}) copy-start(s32[1,16]{1,0:T(1,128)} %param.15) | copy-start | bytes 196
  2.2 34.8 %copy-start.5 = (bf16[180,540]{1,0:T(8,128)(2,1)S(1)}, bf16[180,540]{1,0:T(8,128)(2,1)}, u32[]{:S(2)}) copy-start(bf16[180,540]{1,0:T(8,128)(2,1)} %param.19) | copy-start | bytes 583204
  3.2 41.7 %collective-permute-start = (bf16[4,256,180]{2,1,0:T(8,128)(2,1)S(1)}, bf16[4,256,180]{2,1,0:T(8,128)(2,1)S(1)}, u32[]{:S(2)}, u32[]{:S(2)}) collective-permute-start(bf16[4,256,180]{2,1,0:T(8,128)(2,1)S(1)} %get-tuple-element.15), channel_id=1, source_target_pairs={{0,28},{4,0},{8,4},{12,8},{16,12},{20,16},{24,20},{28,24},{1,29},{... | collective-permute-start | bytes 1105928 | tf_op jit(solution)/shard_map/ppermute | solution.py:220
  9.2 35.7 %collective-permute-start.1 = (bf16[4,256,180]{2,1,0:T(8,128)(2,1)S(1)}, bf16[4,256,180]{2,1,0:T(8,128)(2,1)S(1)}, u32[]{:S(2)}, u32[]{:S(2)}) collective-permute-start(bf16[4,256,180]{2,1,0:T(8,128)(2,1)S(1)} %get-tuple-element.14), channel_id=1, source_target_pairs={{0,4},{4,8},{8,12},{12,16},{16,20},{20,24},{24,28},{28,0},{1,5},{5... | collective-permute-start | bytes 1105928 | tf_op jit(solution)/shard_map/ppermute | solution.py:221
  37.1 3.8 %copy-start.7 = (bf16[180,180]{1,0:T(8,128)(2,1)S(1)}, bf16[180,180]{1,0:T(8,128)(2,1)}, u32[]{:S(2)}) copy-start(bf16[180,180]{1,0:T(8,128)(2,1)} %param.20) | copy-start | bytes 194404
  38.0 4.3 %copy-start.6 = (bf16[360,180]{0,1:T(8,128)(2,1)S(1)}, bf16[360,180]{0,1:T(8,128)(2,1)}, u32[]{:S(2)}) copy-start(bf16[360,180]{0,1:T(8,128)(2,1)} %param.23) | copy-start | bytes 388804
  44.9 0.8 copy-start.3
  44.9 1.0 copy-start.4
  84.1 4.1 %copy-start.2 = (bf16[8,256,180]{2,1,0:T(8,128)(2,1)S(1)}, bf16[8,256,180]{2,1,0:T(8,128)(2,1)}, u32[]{:S(2)}) copy-start(bf16[8,256,180]{2,1,0:T(8,128)(2,1)} %get-tuple-element.12) | copy-start | bytes 2211844
  84.1 21.0 %all-to-all-start = ((bf16[8,2,128,180]{2,1,3,0:T(2,128)(2,1)}), bf16[8,2,128,180]{2,1,3,0:T(2,128)(2,1)S(1)}, u32[]{:S(2)}, u32[]{:S(2)}) async-start(bf16[8,2,128,180]{2,1,3,0:T(2,128)(2,1)} %copy.42), calls=%async_computation | async-start | bytes 1474560 | tf_op jit(solution)/shard_map/all_to_all | solution.py:267

commit v2 on v1

v2 whole, which is shorter than its diff:
```python
import jax
import jax.numpy as jnp
from jax import lax
from jax.experimental import pallas as pl
from jax.experimental.pallas import tpu as pltpu
from jax.sharding import PartitionSpec as P

CHAN = 180
HEADS = 6
WIN = 8
TILE = 2
SHIFT = 4
CAP = 8
TOK = WIN * WIN
HALF = TOK // 2
HEAD_DIM = CHAN // HEADS
GROUP = 4
LANES = 128
SLOT_LANE = 120

EPSILON = 1e-05
BF = jnp.bfloat16
F32 = jnp.float32


def layer_norm(values, gain_vec):
    center = values - jnp.sum(values, axis=-1, keepdims=True) * (1.0 / CHAN)
    spread = jnp.sum(center * center, axis=-1, keepdims=True) * (1.0 / CHAN)
    return (center * lax.rsqrt(spread + EPSILON) * gain_vec).astype(BF)


def dot(a, b):
    return jnp.dot(a, b, preferred_element_type=F32)


def dot_t(a, b):
    return lax.dot_general(a, b, (((1,), (1,)), ((), ())), preferred_element_type=F32)


def biases(bias_ref, last_row, queries):
    first = TOK - queries
    base = jnp.concatenate([bias_ref[h][first:] for h in range(HEADS)], axis=0)
    shape = (HEADS * queries, TOK)
    key = lax.broadcasted_iota(jnp.int32, shape, 1)
    query = lax.broadcasted_iota(jnp.int32, shape, 0) % queries + first
    rows_differ = (key // WIN >= SHIFT) != (query // WIN >= SHIFT)
    cols_differ = (key % WIN >= SHIFT) != (query % WIN >= SHIFT)
    row_pen = jnp.where(rows_differ, jnp.where(last_row, -100.0, 0.0).astype(F32), 0.0)
    plain = base + row_pen
    both = base + jnp.where(cols_differ, -100.0, row_pen)
    return plain, both


def head_masks():
    lane = lax.broadcasted_iota(jnp.int32, (1, CHAN), 1)
    return [
        ((lane >= h * HEAD_DIM) & (lane < (h + 1) * HEAD_DIM)).astype(F32) for h in range(HEADS)
    ]


def attend(x, gain, wq, wk, wv, wp, bias_of, queries):
    masks = head_masks()
    low_masks = [m.astype(BF) for m in masks]
    normed = layer_norm(x, gain)
    if queries == TOK:
        x_q, n_q = x, normed
    else:
        pick = lambda a: jnp.concatenate(
            [a[g * TOK + TOK - queries : (g + 1) * TOK] for g in range(GROUP)], axis=0
        )
        x_q, n_q = pick(x), pick(normed)
    q = (dot(n_q, wq) * HEAD_DIM ** (-0.5)).astype(BF)
    k = dot(normed, wk).astype(BF)
    v = dot(normed, wv).astype(BF)
    mixed = []
    for g in range(GROUP):
        q_w = q[g * queries : (g + 1) * queries]
        stacked = jnp.concatenate([q_w * low_masks[h] for h in range(HEADS)], axis=0)
        scores = dot_t(stacked, k[g * TOK : (g + 1) * TOK]) + bias_of(g)
        top = jnp.max(scores, axis=1, keepdims=True)
        grown = jnp.exp(scores - top)
        weights = (grown * (1.0 / jnp.sum(grown, axis=1, keepdims=True))).astype(BF)
        wide = dot(weights, v[g * TOK : (g + 1) * TOK])
        total = wide[:queries] * masks[0]
        for h in range(1, HEADS):
            total = total + wide[h * queries : (h + 1) * queries] * masks[h]
        mixed.append(total)
    mixed = jnp.concatenate(mixed, axis=0).astype(BF)
    return (x_q + dot(mixed, wp)).astype(BF)


def feed(states, gain, wh, wo):
    flat = states.astype(F32)
    normed = layer_norm(flat, gain)
    inner = jax.nn.gelu(dot(normed, wh)).astype(BF)
    return (flat + dot(inner, wo)).astype(BF)


def roll_cols(x, by):
    by = by % x.shape[1]
    return jnp.concatenate([x[:, by:], x[:, :by]], axis=1)


def window_at(shifted, i, g, row):
    start = pl.multiple_of((i * GROUP + g) * WIN, WIN)
    return shifted[row : row + WIN, pl.ds(start, WIN), :].reshape(TOK, CHAN)


def group_at(shifted, i):
    return jnp.concatenate([window_at(shifted, i, g, 0) for g in range(GROUP)], axis=0)


def own_kernel(
    keep, count, dests, slots, pixels, nxt, bias, gain_a, wq, wk, wv, wp,
    upper, outgoing,
    shifted, first, rest, bias_own, order,
):
    bands = lax.axis_size("band")
    me = lax.axis_index("band")
    windows = pixels.shape[1] // WIN
    tiles = windows // TILE
    pairs = -(-tiles // bands)

    def scan(w, kept):
        order[kept] = w
        return kept + keep[w]

    live = jnp.minimum(lax.fori_loop(0, windows, scan, jnp.int32(0)), count[0])
    shifted[0 : WIN - SHIFT] = roll_cols(pixels[SHIFT:].astype(F32), SHIFT)
    shifted[WIN - SHIFT :] = roll_cols(nxt[...].astype(F32), SHIFT)
    bias_own[0], bias_own[1] = biases(bias, me == bands - 1, TOK)

    def step(i, _):
        def edge(g):
            return bias_own[(i * GROUP + g == windows - 1).astype(jnp.int32)]

        own = attend(group_at(shifted, i), gain_a[...], wq[...], wk[...], wv[...], wp[...], edge, TOK)
        for g in range(GROUP):
            w = i * GROUP + g
            value = own[g * TOK : (g + 1) * TOK]
            upper[w] = value[:HALF]
            first[w] = value[:, :LANES]
            rest[w, :, : CHAN - LANES] = value[:, LANES:].astype(F32)
        return 0

    lax.fori_loop(0, windows // GROUP, step, 0)
    if bands * pairs > tiles:
        outgoing[...] = jnp.full(outgoing.shape, CAP, BF)
    lane = lax.broadcasted_iota(jnp.int32, (TOK, LANES), 1)

    def pack(t, _):
        place = dests[t] * pairs + t // bands
        slot = jnp.where(t * TILE < live, slots[t], CAP).astype(F32)
        halves = []
        for p in range(TILE):
            position = t * TILE + p
            valid = position < live
            source = jnp.where(valid, order[jnp.where(valid, position, 0)], 0)
            value = first[source]
            outgoing[place, p * TOK : (p + 1) * TOK] = jnp.where(valid, value, jnp.zeros_like(value))
            tail = rest[source]
            halves.append(jnp.where(valid & (lane < CHAN - LANES), tail, 0.0))
        both = jnp.where(lane < TOK, halves[0], pltpu.roll(halves[1], TOK, 1))
        both = jnp.where(lane >= SLOT_LANE, slot, both)
        outgoing[place, TILE * TOK :] = both.astype(BF)
        return 0

    lax.fori_loop(0, tiles, pack, 0)


def map_kernel(
    keep_own, keep_prev, counts, pixels, prv, upper, bias, gain_a, wq, wk, wv, wp, gain_m, wh, wo,
    restored,
    shifted, result, bias_prev, act_own, act_prev,
):
    me = lax.axis_index("band")
    windows = pixels.shape[1] // WIN

    def scan(w, carry):
        own, prev = carry
        act_own[w] = ((keep_own[w] == 1) & (own < counts[0])).astype(jnp.int32)
        act_prev[w] = ((keep_prev[w] == 1) & (prev < counts[1])).astype(jnp.int32)
        return own + keep_own[w], prev + keep_prev[w]

    lax.fori_loop(0, windows, scan, (jnp.int32(0), jnp.int32(0)))
    shifted[0:SHIFT] = roll_cols(prv[...].astype(F32), SHIFT)
    shifted[SHIFT:] = roll_cols(pixels[...].astype(F32), SHIFT)
    bias_prev[0], bias_prev[1] = biases(bias, me == 0, HALF)

    def step(i, _):
        def edge(g):
            return bias_prev[(i * GROUP + g == windows - 1).astype(jnp.int32)]

        prev = attend(group_at(shifted, i), gain_a[...], wq[...], wk[...], wv[...], wp[...], edge, HALF)
        states = jnp.concatenate([upper[i * GROUP + g] for g in range(GROUP)] + [prev], axis=0)
        done = feed(states, gain_m[...], wh[...], wo[...]).astype(F32)
        for g in range(GROUP):
            w = i * GROUP + g
            cols = pl.ds(pl.multiple_of(w * WIN, WIN), WIN)
            upper_new = done[g * HALF : (g + 1) * HALF].reshape(SHIFT, WIN, CHAN)
            lower_new = done[(GROUP + g) * HALF : (GROUP + g + 1) * HALF].reshape(SHIFT, WIN, CHAN)
            result[0:SHIFT, cols, :] = jnp.where(
                act_prev[w] == 1, lower_new, shifted[SHIFT : 2 * SHIFT, cols, :]
            )
            result[SHIFT:, cols, :] = jnp.where(
                act_own[w] == 1, upper_new, shifted[2 * SHIFT :, cols, :]
            )
        return 0

    lax.fori_loop(0, windows // GROUP, step, 0)
    restored[...] = roll_cols(result[...], -SHIFT).astype(BF)


def place_kernel(incoming, work):
    work[...] = jnp.zeros(work.shape, BF)
    lane = lax.broadcasted_iota(jnp.int32, (16, LANES), 1)

    def put(t, _):
        head = incoming[t, TILE * TOK : TILE * TOK + 16].astype(F32)
        slot = jnp.max(jnp.where(lane >= SLOT_LANE, head, 0.0)).astype(jnp.int32)

        @pl.when(slot < CAP)
        def _():
            tail = incoming[t, TILE * TOK :].astype(F32)
            work[slot, :, :LANES] = incoming[t, : TILE * TOK]
            work[slot, :TOK, LANES:] = tail[:, : CHAN - LANES].astype(BF)
            work[slot, TOK:, LANES:] = pltpu.roll(tail, TOK, 1)[:, : CHAN - LANES].astype(BF)

        return 0

    lax.fori_loop(0, incoming.shape[0], put, 0)


def position_bias(bias_table):
    coords = jnp.arange(TOK, dtype=jnp.int32)
    row_pos, col_pos = coords // WIN, coords % WIN
    index = (row_pos[:, None] - row_pos[None, :] + WIN - 1) * (2 * WIN - 1) + (
        col_pos[:, None] - col_pos[None, :] + WIN - 1
    )
    entries = bias_table.shape[0]
    onehot = (jnp.arange(entries, dtype=jnp.int32)[:, None] == index.reshape(1, -1)).astype(F32)
    return jnp.dot(bias_table.T, onehot, precision=lax.Precision.HIGHEST).reshape(HEADS, TOK, TOK)


def shards(
    pixels, keep_mask, band_counts, plan_dest, plan_slot, bias_table, gain_attn, qkv_weight,
    proj_weight, gain_mlp, hidden_weight, output_weight,
):
    bands = lax.axis_size("band")
    rows, cols, channels = pixels.shape
    windows = cols // WIN
    tiles = windows // TILE
    pairs = -(-tiles // bands)
    ahead = [(s, (s + 1) % bands) for s in range(bands)]
    back = [(s, (s - 1) % bands) for s in range(bands)]
    turned = jnp.transpose(pixels, (2, 0, 1))
    nxt = jnp.transpose(lax.ppermute(turned[:, :SHIFT], "band", back), (1, 2, 0))
    prv = jnp.transpose(lax.ppermute(turned[:, rows - SHIFT :], "band", ahead), (1, 2, 0))
    facts = lax.ppermute(jnp.concatenate([keep_mask[0], band_counts]), "band", ahead)
    keep_prev = facts[:windows]
    counts = jnp.concatenate([band_counts, facts[windows:]])

    bias = position_bias(bias_table)
    wq, wk, wv = (qkv_weight[:, i * CHAN : (i + 1) * CHAN] for i in range(3))
    smem = pl.BlockSpec(memory_space=pltpu.SMEM)
    vmem = pl.BlockSpec(memory_space=pltpu.VMEM)
    limit = pltpu.CompilerParams(vmem_limit_bytes=40 * 1024 * 1024)
    upper, outgoing = pl.pallas_call(
        own_kernel,
        out_shape=(
            jax.ShapeDtypeStruct((windows, HALF, channels), BF),
            jax.ShapeDtypeStruct((bands * pairs, TILE * TOK + TOK, LANES), BF),
        ),
        in_specs=[smem] * 4 + [vmem] * 8,
        out_specs=(vmem, vmem),
        scratch_shapes=[
            pltpu.VMEM((rows, cols, channels), F32),
            pltpu.VMEM((windows, TOK, LANES), BF),
            pltpu.VMEM((windows, TOK, LANES), F32),
            pltpu.VMEM((2, HEADS * TOK, TOK), F32),
            pltpu.SMEM((windows + 1,), jnp.int32),
        ],
        compiler_params=limit,
        cost_estimate=pl.CostEstimate(flops=3 * 10**9, bytes_accessed=10**7, transcendentals=10**6),
        name="own",
    )(
        keep_mask[0], band_counts, plan_dest[0], plan_slot[0],
        pixels, nxt, bias, gain_attn[None], wq, wk, wv, proj_weight,
    )
    incoming = lax.all_to_all(
        outgoing.reshape(bands, -1, LANES), "band", split_axis=0, concat_axis=0, tiled=True
    ).reshape(outgoing.shape)
    restored = pl.pallas_call(
        map_kernel,
        out_shape=jax.ShapeDtypeStruct((rows, cols, channels), BF),
        in_specs=[smem] * 3 + [vmem] * 12,
        out_specs=vmem,
        scratch_shapes=[
            pltpu.VMEM((rows + SHIFT, cols, channels), F32),
            pltpu.VMEM((rows, cols, channels), F32),
            pltpu.VMEM((2, HEADS * HALF, TOK), F32),
            pltpu.SMEM((windows,), jnp.int32),
            pltpu.SMEM((windows,), jnp.int32),
        ],
        compiler_params=limit,
        cost_estimate=pl.CostEstimate(flops=10**10, bytes_accessed=3 * 10**7, transcendentals=10**6),
        name="map",
    )(
        keep_mask[0], keep_prev, counts, pixels, prv, upper, bias, gain_attn[None], wq, wk, wv,
        proj_weight, gain_mlp[None], hidden_weight, output_weight,
    )
    work = pl.pallas_call(
        place_kernel,
        out_shape=jax.ShapeDtypeStruct((CAP, TILE * TOK, channels), BF),
        in_specs=[vmem],
        out_specs=vmem,
        compiler_params=limit,
        name="place",
    )(incoming)
    return restored, work


def solution(mesh):
    split = P(("img", "band"))
    in_specs = (split,) * 5 + (P(),) * 7
    return jax.shard_map(shards, mesh=mesh, in_specs=in_specs, out_specs=(split, split), check_vma=False)
```

time: 107 us -> 101 us (0.944)
  blocking collectives: 25.7 us -> 0 us
  waiting for transfers between devices: 15.5 us -> 33.4 us
  starting transfers between devices: 9.68 us -> 16.1 us
  Pallas kernels: 35.1 us -> 33.4 us
  local copies, waits for them, and re-layouts: 15.3 us -> 14 us
  other arithmetic: 2.05 us -> 0.87 us
    ppermute x2 -> x3, waiting for transfers between devices: 0.01 us -> 33.4 us  [the longest x1 24.6 us: shards(): lax.ppermute(jnp.concatenate([keep_mask[0], band_counts]), 'band', ahead)]
    unnamed x1 -> x0, blocking collectives: 25.7 us -> none
    all_to_all x1, waiting for transfers between devices: 15.5 us -> 0.01 us  [shards(): lax.all_to_all(outgoing.reshape(bands, -1, LANES), 'band', split_axis=0,...]
    unnamed x30 -> x42, local copies, waits for them, and re-layouts: 6.94 us -> 12.2 us
    reshape x4 -> x1, local copies, waits for them, and re-layouts: 4 us -> 0.09 us  [position_bias(): jnp.dot(bias_table.T, onehot, precision=lax.Precision.HIGHEST)]
    ppermute x2 -> x3, starting transfers between devices: 6.01 us -> 9.54 us  [the longest x1 6.06 us: shards(): lax.ppermute(turned[:, :SHIFT], 'band', back)]
    all_to_all x1, starting transfers between devices: 3.68 us -> 6.59 us  [shards(): lax.all_to_all(outgoing.reshape(bands, -1, LANES), 'band', split_axis=0,...]
    pallas_call x1 -> x3, Pallas kernels: 35.1 us -> 33.4 us  [the longest x1 15.7 us: shards(): pl.pallas_call(own_kernel, out_shape=(jax.ShapeDtypeStruct((windows, HALF...]
  transfers between devices with their start and end apart: 3 -> 4, of which waited for: 1 -> 2; matrix products, arithmetic and copies ran while one was open for 10% -> 5% of each run, Pallas kernels for 0% -> 15%
where the time goes in v2:
time: 101 us
  waiting for transfers between devices  33.4 us (33%)
  Pallas kernels  33.4 us (33%)
  starting transfers between devices  16.1 us (16%)
  local copies, waits for them, and re-layouts  14 us (14%)
  between operations  1.4 us (1%)
  matrix products  1.3 us (1%)
    ppermute x1, waiting for transfers between devices, shards(): lax.ppermute(jnp.concatenate([keep_mask[0], band_counts]), 'band', ahead)  24.6 us
    pallas_call x1, Pallas kernels, shards(): pl.pallas_call(own_kernel, out_shape=(jax.ShapeDtypeStruct((windows, HALF...  15.7 us
    pallas_call x1, Pallas kernels, shards(): pl.pallas_call(map_kernel, out_shape=jax.ShapeDtypeStruct((rows, cols, ch...  15 us
    unnamed x42, local copies, waits for them, and re-layouts  12.2 us
    ppermute x1, waiting for transfers between devices, shards(): lax.ppermute(turned[:, :SHIFT], 'band', back)  8.83 us
    all_to_all x1, starting transfers between devices, shards(): lax.all_to_all(outgoing.reshape(bands, -1, LANES), 'band', split_axis=0,...  6.59 us
    ppermute x1, starting transfers between devices, shards(): lax.ppermute(turned[:, :SHIFT], 'band', back)  6.06 us
    pallas_call x1, Pallas kernels, shards(): pl.pallas_call(place_kernel, out_shape=jax.ShapeDtypeStruct((CAP, TILE *...  2.68 us
  transfers between devices with their start and end apart: 4, of which 2 were waited for; matrix products, arithmetic and copies ran while one was open for 5% of the time, Pallas kernels for 15%

profile of v2, /device:TPU:0, one launch (start us, length us, event | category | flops | bytes accessed | tf_op | source)
XLA Modules:
  0.0 100.5 jit_solution(2491508133062334349)
XLA Ops:
  0.6 1.5 %copy.16.pixels = bf16[8,256,180]{2,1,0:T(8,128)(2,1)S(1)} copy(bf16[8,256,180]{1,0,2:T(8,128)(2,1)} %param.12) | data formatting | bytes 1474560 | tf_op args[0]
  2.2 0.9 fusion.1
  3.1 6.1 %collective-permute-start.2 = (bf16[180,4,256]{0,2,1:T(8,128)(2,1)S(1)}, bf16[180,4,256]{0,2,1:T(8,128)(2,1)S(1)}, u32[]{:S(2)}, u32[]{:S(2)}) collective-permute-start(bf16[180,4,256]{0,2,1:T(8,128)(2,1)S(1)} %get-tuple-element.8), channel_id=1, source_target_pairs={{0,28},{4,0},{8,4},{12,8},{16,12},{20,16},{24,20},{28,24},{1,29},{... | collective-permute-start | bytes 1105928 | tf_op jit(solution)/shard_map/ppermute | solution.py:257
  9.8 0.1 add_add_fusion
  9.9 0.1 add.55
  10.0 1.3 %convolution_bitcast_fusion = f32[6,4096]{1,0:T(8,128)S(1)} fusion(f32[225,6]{0,1:T(8,128)S(1)} %copy-done, s32[4096]{0:T(1024)S(1)} %add.55), kind=kOutput, calls=%fused_computation | convolution fusion | flops 67276800 | bytes 120088 | tf_op jit(solution)/shard_map/dot_general | solution.py:242
  11.3 0.1 reshape.97.bias
  11.4 0.1 fusion.2
  11.5 8.8 %collective-permute-done.2 = bf16[180,4,256]{0,2,1:T(8,128)(2,1)S(1)} collective-permute-done((bf16[180,4,256]{0,2,1:T(8,128)(2,1)S(1)}, bf16[180,4,256]{0,2,1:T(8,128)(2,1)S(1)}, u32[]{:S(2)}, u32[]{:S(2)}) %collective-permute-start.2) | collective-permute-done | bytes 368672 | tf_op jit(solution)/shard_map/ppermute | solution.py:257
  20.3 15.7 %own.1 = (bf16[32,32,180]{2,1,0:T(8,128)(2,1)S(1)}, bf16[16,192,128]{2,1,0:T(8,128)(2,1)}) custom-call(s32[32]{0:T(128)S(1)} %bitcast.23, s32[1]{0:T(128)S(6)} %copy.20.count, s32[16]{0:T(128)S(1)} %bitcast.21, s32[16]{0:T(128)S(1)} %bitcast.22, bf16[8,256,180]{2,1,0:T(8,128)(2,1)S(1)} %copy.16.pixels, bf16[4,256,180]{2,1,0:T(8,128)(2,1)S(1)} %bitcast.16, ...), custom_call_target="tpu_custom_call" | custom-call | flops 3000000000 | bytes 10000000 | tf_op jit(solution)/shard_map/own/pallas_call | solution.py:268
  36.1 0.8 copy-done.15
  36.9 6.6 %all-to-all-start = ((bf16[8,384,128]{2,1,0:T(8,128)(2,1)}), bf16[8,384,128]{2,1,0:T(8,128)(2,1)S(1)}, u32[]{:S(2)}, u32[]{:S(2)}) async-start(bf16[8,384,128]{2,1,0:T(8,128)(2,1)} %bitcast.9), calls=%async_computation | async-start | bytes 1572864 | tf_op jit(solution)/shard_map/all_to_all | solution.py:290
  43.5 2.0 %collective-permute-start.1 = (bf16[180,4,256]{0,2,1:T(8,128)(2,1)}, bf16[180,4,256]{0,2,1:T(8,128)(2,1)S(1)}, u32[]{:S(2)}, u32[]{:S(2)}) collective-permute-start(bf16[180,4,256]{0,2,1:T(8,128)(2,1)} %get-tuple-element.9), channel_id=1, source_target_pairs={{0,4},{4,8},{8,12},{12,16},{16,20},{20,24},{24,28},{28,0},{1,5},{5... | collective-permute-start | bytes 1105928 | tf_op jit(solution)/shard_map/ppermute | solution.py:258
  45.5 0.1 pad_add_fusion
  45.6 1.5 %collective-permute-start = (s32[33]{0:T(128)S(1)}, s32[33]{0:T(128)S(1)}, u32[]{:S(2)}, u32[]{:S(2)}) collective-permute-start(s32[33]{0:T(128)S(1)} %pad_add_fusion), channel_id=1, source_target_pairs={{0,4},{4,8},{8,12},{12,16},{16,20},{20,24},{24,28},{28,0},{1,5},{5... | collective-permute-start | bytes 404 | tf_op jit(solution)/shard_map/ppermute | solution.py:259
  47.0 0.1 copy.17.wo
  47.2 24.6 %collective-permute-done = s32[33]{0:T(128)S(1)} collective-permute-done((s32[33]{0:T(128)S(1)}, s32[33]{0:T(128)S(1)}, u32[]{:S(2)}, u32[]{:S(2)}) %collective-permute-start) | collective-permute-done | bytes 164 | tf_op jit(solution)/shard_map/ppermute | solution.py:259
  71.8 0.6 slice.22
  72.4 0.7 pad_add_fusion.1.counts
  73.1 0.8 copy-done.1
  73.9 1.0 %copy-done.2 = bf16[180,4,256]{0,2,1:T(8,128)(2,1)S(1)} copy-done((bf16[180,4,256]{0,2,1:T(8,128)(2,1)S(1)}, bf16[180,4,256]{0,2,1:T(8,128)(2,1)}, u32[]{:S(2)}) %copy-start.2) | copy-done | bytes 368664
  74.9 0.9 copy-done.3
  75.8 0.9 copy-done.5
  76.7 0.7 copy-done.7
  77.4 0.7 copy-done.8
  78.1 0.7 copy-done.12
  78.8 0.7 copy-done.14
  79.4 1.0 %copy-done.16 = bf16[32,32,180]{2,1,0:T(8,128)(2,1)S(1)} copy-done((bf16[32,32,180]{2,1,0:T(8,128)(2,1)S(1)}, bf16[32,32,180]{2,1,0:T(8,128)(2,1)}, u32[]{:S(2)}) %copy-start.16) | copy-done | bytes 368664
  80.4 15.0 %map.1 = bf16[8,256,180]{2,1,0:T(8,128)(2,1)S(1)} custom-call(s32[32]{0:T(128)S(1)} %bitcast.25, s32[32]{0:T(128)S(1)} %bitcast.26, s32[2]{0:T(128)S(1)} %pad_add_fusion.1.counts, bf16[8,256,180]{2,1,0:T(8,128)(2,1)S(1)} %copy.16.pixels, bf16[4,256,180]{2,1,0:T(8,128)(2,1)S(1)} %bitcast.17, bf16[32,32,180]{2,1,0:T(8,128)(2,1)S(1)} %copy-done.16, ...), custom_call_target="tpu_custom_call" | custom-call | flops 10000000000 | bytes 30000000 | tf_op jit(solution)/shard_map/map/pallas_call | solution.py:293
  95.5 1.4 %copy.18 = bf16[8,256,180]{1,0,2:T(8,128)(2,1)} copy(bf16[8,256,180]{2,1,0:T(8,128)(2,1)S(1)} %map.1) | data formatting | bytes 1474560
  96.8 2.7 %place.1 = bf16[8,128,180]{2,1,0:T(8,128)(2,1)S(1)} custom-call(bf16[16,192,128]{2,1,0:T(8,128)(2,1)S(1)} %bitcast.15), custom_call_target="tpu_custom_call" | custom-call | tf_op jit(solution)/shard_map/place/pallas_call | solution.py:312
  99.5 1.0 copy.19
  (31 shorter events, 0.1 us)
Async XLA Ops:
  0.6 9.3 %copy-start = (f32[225,6]{0,1:T(8,128)S(1)}, f32[225,6]{0,1:T(8,128)}, u32[]{:S(2)}) copy-start(f32[225,6]{0,1:T(8,128)} %param.17) | copy-start | bytes 16204
  3.0 8.3 %copy-start.17 = (bf16[180,540]{1,0:T(8,128)(2,1)S(1)}, bf16[180,540]{1,0:T(8,128)(2,1)}, u32[]{:S(2)}) copy-start(bf16[180,540]{1,0:T(8,128)(2,1)} %param.19) | copy-start | bytes 583204
  3.1 17.3 %copy-start.4 = (bf16[180,180]{1,0:T(8,128)(2,1)S(1)}, bf16[180,180]{1,0:T(8,128)(2,1)}, u32[]{:S(2)}) copy-start(bf16[180,180]{1,0:T(8,128)(2,1)} %wp.3) | copy-start | bytes 194404
  3.1 17.3 %copy-start.6 = (f32[180]{0:T(256)S(1)}, f32[180]{0:T(256)}, u32[]{:S(2)}) copy-start(f32[180]{0:T(256)} %param.18) | copy-start | bytes 2164
  3.1 17.3 %copy-start.9 = (s32[1,16]{1,0:T(1,128)S(1)}, s32[1,16]{1,0:T(1,128)}, u32[]{:S(2)}) copy-start(s32[1,16]{1,0:T(1,128)} %param.15) | copy-start | bytes 196
  3.1 17.3 %copy-start.10 = (s32[1,16]{1,0:T(1,128)S(1)}, s32[1,16]{1,0:T(1,128)}, u32[]{:S(2)}) copy-start(s32[1,16]{1,0:T(1,128)} %param.16) | copy-start | bytes 196
  3.1 17.3 %copy-start.11 = (s32[1,32]{1,0:T(1,128)S(1)}, s32[1,32]{1,0:T(1,128)}, u32[]{:S(2)}) copy-start(s32[1,32]{1,0:T(1,128)} %param.13) | copy-start | bytes 388
  3.1 17.2 %collective-permute-start.2 = (bf16[180,4,256]{0,2,1:T(8,128)(2,1)S(1)}, bf16[180,4,256]{0,2,1:T(8,128)(2,1)S(1)}, u32[]{:S(2)}, u32[]{:S(2)}) collective-permute-start(bf16[180,4,256]{0,2,1:T(8,128)(2,1)S(1)} %get-tuple-element.8), channel_id=1, source_target_pairs={{0,28},{4,0},{8,4},{12,8},{16,12},{20,16},{24,20},{28,24},{1,29},{... | collective-permute-start | bytes 1105928 | tf_op jit(solution)/shard_map/ppermute | solution.py:257
  36.1 0.8 copy-start.15
  36.9 10.2 %copy-start.18 = (bf16[360,180]{0,1:T(8,128)(2,1)S(1)}, bf16[360,180]{0,1:T(8,128)(2,1)}, u32[]{:S(2)}) copy-start(bf16[360,180]{0,1:T(8,128)(2,1)} %param.23) | copy-start | bytes 388804
  36.9 59.9 %all-to-all-start = ((bf16[8,384,128]{2,1,0:T(8,128)(2,1)}), bf16[8,384,128]{2,1,0:T(8,128)(2,1)S(1)}, u32[]{:S(2)}, u32[]{:S(2)}) async-start(bf16[8,384,128]{2,1,0:T(8,128)(2,1)} %bitcast.9), calls=%async_computation | async-start | bytes 1572864 | tf_op jit(solution)/shard_map/all_to_all | solution.py:290
  43.5 29.6 %collective-permute-start.1 = (bf16[180,4,256]{0,2,1:T(8,128)(2,1)}, bf16[180,4,256]{0,2,1:T(8,128)(2,1)S(1)}, u32[]{:S(2)}, u32[]{:S(2)}) collective-permute-start(bf16[180,4,256]{0,2,1:T(8,128)(2,1)} %get-tuple-element.9), channel_id=1, source_target_pairs={{0,4},{4,8},{8,12},{12,16},{16,20},{20,24},{24,28},{28,0},{1,5},{5... | collective-permute-start | bytes 1105928 | tf_op jit(solution)/shard_map/ppermute | solution.py:258
  45.6 26.2 %collective-permute-start = (s32[33]{0:T(128)S(1)}, s32[33]{0:T(128)S(1)}, u32[]{:S(2)}, u32[]{:S(2)}) collective-permute-start(s32[33]{0:T(128)S(1)} %pad_add_fusion), channel_id=1, source_target_pairs={{0,4},{4,8},{8,12},{12,16},{16,20},{20,24},{24,28},{28,0},{1,5},{5... | collective-permute-start | bytes 404 | tf_op jit(solution)/shard_map/ppermute | solution.py:259
  71.8 2.1 %copy-start.13 = (s32[33]{0:T(128)}, s32[33]{0:T(128)S(1)}, u32[]{:S(2)}) copy-start(s32[33]{0:T(128)S(1)} %collective-permute-done) | copy-start | bytes 400
  73.1 0.8 copy-start.1
  73.9 1.0 %copy-start.2 = (bf16[180,4,256]{0,2,1:T(8,128)(2,1)S(1)}, bf16[180,4,256]{0,2,1:T(8,128)(2,1)}, u32[]{:S(2)}) copy-start(bf16[180,4,256]{0,2,1:T(8,128)(2,1)} %copy-done.1) | copy-start | bytes 1105924
  74.9 0.9 copy-start.3
  75.8 0.9 copy-start.5
  76.7 0.7 copy-start.7
  77.4 0.7 copy-start.8
  78.1 0.7 copy-start.12
  78.7 0.7 copy-start.14
  79.4 1.0 %copy-start.16 = (bf16[32,32,180]{2,1,0:T(8,128)(2,1)S(1)}, bf16[32,32,180]{2,1,0:T(8,128)(2,1)}, u32[]{:S(2)}) copy-start(bf16[32,32,180]{2,1,0:T(8,128)(2,1)} %copy-done.15) | copy-start | bytes 1105924

commit v3 on v2

--- a/solution.py
+++ b/solution.py
@@ -257,14 +257,14 @@
     nxt = jnp.transpose(lax.ppermute(turned[:, :SHIFT], "band", back), (1, 2, 0))
     prv = jnp.transpose(lax.ppermute(turned[:, rows - SHIFT :], "band", ahead), (1, 2, 0))
     facts = lax.ppermute(jnp.concatenate([keep_mask[0], band_counts]), "band", ahead)
+    bias = position_bias(bias_table)
+    nxt, prv, facts, bias = lax.optimization_barrier((nxt, prv, facts, bias))
     keep_prev = facts[:windows]
     counts = jnp.concatenate([band_counts, facts[windows:]])
-
-    bias = position_bias(bias_table)
     wq, wk, wv = (qkv_weight[:, i * CHAN : (i + 1) * CHAN] for i in range(3))
     smem = pl.BlockSpec(memory_space=pltpu.SMEM)
     vmem = pl.BlockSpec(memory_space=pltpu.VMEM)
-    limit = pltpu.CompilerParams(vmem_limit_bytes=40 * 1024 * 1024)
+    limit = pltpu.CompilerParams(vmem_limit_bytes=63 * 1024 * 1024)
     upper, outgoing = pl.pallas_call(
         own_kernel,
         out_shape=(

time: 101 us -> 85.7 us (0.85)
  waiting for transfers between devices: 33.4 us -> 18.1 us
  Pallas kernels: 33.4 us -> 38.7 us
  starting transfers between devices: 16.1 us -> 12.2 us
  local copies, waits for them, and re-layouts: 14 us -> 11.7 us
  other arithmetic: 0.87 us -> 2.03 us
    ppermute x1, waiting for transfers between devices: 24.6 us -> 0.01 us  [shards(): lax.ppermute(jnp.concatenate([keep_mask[0], band_counts]), 'band', ahead)]
    ppermute x1, waiting for transfers between devices: 0.01 us -> 15.9 us  [shards(): lax.ppermute(turned[:, rows - SHIFT:], 'band', ahead)]
    ppermute x1, waiting for transfers between devices: 8.83 us -> 2.2 us  [shards(): lax.ppermute(turned[:, :SHIFT], 'band', back)]
    unnamed x42 -> x20, local copies, waits for them, and re-layouts: 12.2 us -> 9.31 us
    ppermute x1, starting transfers between devices: 6.06 us -> 3.17 us  [shards(): lax.ppermute(turned[:, :SHIFT], 'band', back)]
    pallas_call x1, Pallas kernels: 15 us -> 17.2 us  [shards(): pl.pallas_call(map_kernel, out_shape=jax.ShapeDtypeStruct((rows, cols, ch...]
    all_to_all x1, starting transfers between devices: 6.59 us -> 4.5 us  [shards(): lax.all_to_all(outgoing.reshape(bands, -1, LANES), 'band', split_axis=0,...]
    pallas_call x1, Pallas kernels: 2.68 us -> 4.63 us  [shards(): pl.pallas_call(place_kernel, out_shape=jax.ShapeDtypeStruct((CAP, TILE *...]
  transfers between devices with their start and end apart: 4 -> 4, of which waited for: 2 -> 2; matrix products, arithmetic and copies ran while one was open for 5% -> 11% of each run, Pallas kernels for 15% -> 20%
where the time goes in v3:
time: 85.7 us; the launch traced here: 85.3 us
  Pallas kernels  38.7 us (45%)
  waiting for transfers between devices  18.1 us (21%)
  starting transfers between devices  12.2 us (14%)
  local copies, waits for them, and re-layouts  11.7 us (14%)
  other arithmetic  2.03 us (2%)
  between operations  1.36 us (2%)
  matrix products  1.3 us (2%)
    pallas_call x1, Pallas kernels, shards(): pl.pallas_call(map_kernel, out_shape=jax.ShapeDtypeStruct((rows, cols, ch...  17.2 us
    pallas_call x1, Pallas kernels, shards(): pl.pallas_call(own_kernel, out_shape=(jax.ShapeDtypeStruct((windows, HALF...  16.8 us
    ppermute x1, waiting for transfers between devices, shards(): lax.ppermute(turned[:, rows - SHIFT:], 'band', ahead)  15.9 us
    unnamed x20, local copies, waits for them, and re-layouts  9.31 us
    pallas_call x1, Pallas kernels, shards(): pl.pallas_call(place_kernel, out_shape=jax.ShapeDtypeStruct((CAP, TILE *...  4.63 us
    all_to_all x1, starting transfers between devices, shards(): lax.all_to_all(outgoing.reshape(bands, -1, LANES), 'band', split_axis=0,...  4.5 us
    ppermute x1, starting transfers between devices, shards(): lax.ppermute(turned[:, :SHIFT], 'band', back)  3.17 us
    ppermute x1, starting transfers between devices, shards(): lax.ppermute(jnp.concatenate([keep_mask[0], band_counts]), 'band', ahead)  2.97 us
  transfers between devices with their start and end apart: 4, of which 2 were waited for; matrix products, arithmetic and copies ran while one was open for 11% of the time, Pallas kernels for 20%

profile of v3, /device:TPU:0, one launch (start us, length us, event | category | flops | bytes accessed | tf_op | source)
XLA Modules:
  0.0 85.3 jit_solution(11810101634664590377)
XLA Ops:
  0.6 0.0 copy-start
  1.3 0.7 pad_add_fusion
  2.0 3.0 %collective-permute-start.2 = (s32[33]{0:T(128)S(1)}, s32[33]{0:T(128)S(1)}, u32[]{:S(2)}, u32[]{:S(2)}) collective-permute-start(s32[33]{0:T(128)S(1)} %pad_add_fusion), channel_id=1, source_target_pairs={{0,4},{4,8},{8,12},{12,16},{16,20},{20,24},{24,28},{28,0},{1,5},{5... | collective-permute-start | bytes 404 | tf_op jit(solution)/shard_map/ppermute | solution.py:259
  5.0 1.5 %copy.14.pixels = bf16[8,256,180]{2,1,0:T(8,128)(2,1)S(1)} copy(bf16[8,256,180]{1,0,2:T(8,128)(2,1)} %param.12) | data formatting | bytes 1474560 | tf_op args[0]
  6.5 0.0 copy-start.1
  6.5 0.0 copy-start.3
  6.6 0.1 fusion.1
  6.6 0.9 %copy-done.1 = bf16[8,256,180]{2,1,0:T(8,128)(2,1)} copy-done((bf16[8,256,180]{2,1,0:T(8,128)(2,1)}, bf16[8,256,180]{2,1,0:T(8,128)(2,1)S(1)}, u32[]{:S(2)}) %copy-start.1) | copy-done | bytes 737304
  7.5 1.5 %collective-permute-start.1 = (bf16[180,4,256]{0,2,1:T(8,128)(2,1)S(1)}, bf16[180,4,256]{0,2,1:T(8,128)(2,1)S(1)}, u32[]{:S(2)}, u32[]{:S(2)}) collective-permute-start(bf16[180,4,256]{0,2,1:T(8,128)(2,1)S(1)} %get-tuple-element.16), channel_id=1, source_target_pairs={{0,4},{4,8},{8,12},{12,16},{16,20},{20,24},{24,28},{28,0},{1,5},{5... | collective-permute-start | bytes 1105928 | tf_op jit(solution)/shard_map/ppermute | solution.py:258
  9.1 3.2 %collective-permute-start = (bf16[180,4,256]{0,2,1:T(8,128)(2,1)S(1)}, bf16[180,4,256]{0,2,1:T(8,128)(2,1)S(1)}, u32[]{:S(2)}, u32[]{:S(2)}) collective-permute-start(bf16[180,4,256]{0,2,1:T(8,128)(2,1)S(1)} %get-tuple-element.17), channel_id=1, source_target_pairs={{0,28},{4,0},{8,4},{12,8},{16,12},{20,16},{24,20},{28,24},{1,29},{... | collective-permute-start | bytes 1105928 | tf_op jit(solution)/shard_map/ppermute | solution.py:257
  12.2 0.1 add_add_fusion
  12.3 0.1 add.55
  12.4 0.0 copy-done.3
  12.4 0.8 fusion.2
  13.2 1.3 %convolution_bitcast_fusion = f32[6,4096]{1,0:T(8,128)S(1)} fusion(f32[225,6]{0,1:T(8,128)S(1)} %copy-done, s32[4096]{0:T(1024)S(1)} %add.55), kind=kOutput, calls=%fused_computation | convolution fusion | flops 67276800 | bytes 120088 | tf_op jit(solution)/shard_map/dot_general | solution.py:242
  14.5 0.8 reshape.97.bias
  15.3 0.0 collective-permute-done.2
  15.3 15.9 %collective-permute-done.1 = bf16[180,4,256]{0,2,1:T(8,128)(2,1)S(1)} collective-permute-done((bf16[180,4,256]{0,2,1:T(8,128)(2,1)S(1)}, bf16[180,4,256]{0,2,1:T(8,128)(2,1)S(1)}, u32[]{:S(2)}, u32[]{:S(2)}) %collective-permute-start.1) | collective-permute-done | bytes 368672 | tf_op jit(solution)/shard_map/ppermute | solution.py:258
  31.2 2.2 %collective-permute-done = bf16[180,4,256]{0,2,1:T(8,128)(2,1)S(1)} collective-permute-done((bf16[180,4,256]{0,2,1:T(8,128)(2,1)S(1)}, bf16[180,4,256]{0,2,1:T(8,128)(2,1)S(1)}, u32[]{:S(2)}, u32[]{:S(2)}) %collective-permute-start) | collective-permute-done | bytes 368672 | tf_op jit(solution)/shard_map/ppermute | solution.py:257
  33.4 0.8 copy-done.6
  34.2 16.8 %own.1 = (bf16[32,32,180]{2,1,0:T(8,128)(2,1)}, bf16[16,192,128]{2,1,0:T(8,128)(2,1)}) custom-call(s32[32]{0:T(128)} %bitcast.25, s32[1]{0:T(128)S(6)} %copy.20.count, s32[16]{0:T(128)} %bitcast.22, s32[16]{0:T(128)} %bitcast.23, bf16[8,256,180]{2,1,0:T(8,128)(2,1)} %copy-done.1, bf16[4,256,180]{2,1,0:T(8,128)(2,1)} %bitcast.18, f32[6,64,64]{2,1,0:T(8,128)} %reshape.97.bias, ...), custom_call_target="tpu_custom_call" | custom-call | flops 3000000000 | bytes 10000000 | tf_op jit(solution)/shard_map/own/pallas_call | solution.py:268
  51.1 4.5 %all-to-all-start = ((bf16[8,384,128]{2,1,0:T(8,128)(2,1)}), bf16[8,384,128]{2,1,0:T(8,128)(2,1)S(1)}, u32[]{:S(2)}, u32[]{:S(2)}) async-start(bf16[8,384,128]{2,1,0:T(8,128)(2,1)} %bitcast.16), calls=%async_computation | async-start | bytes 1572864 | tf_op jit(solution)/shard_map/all_to_all | solution.py:290
  55.6 0.0 copy-done.4
  55.6 0.8 copy.17.wo
  56.4 0.6 slice.24
  57.0 1.2 %pad_add_fusion.1.counts = s32[2]{0:T(128)} fusion(s32[1]{0:T(128)} %slice.24, s32[1]{0:T(128)S(6)} %copy.20.count), kind=kLoop, calls=%fused_computation.10 | loop fusion | flops 2 | bytes 16 | tf_op jit(solution)/shard_map/concatenate | solution.py:263
  58.2 17.2 %map.1 = bf16[8,256,180]{2,1,0:T(8,128)(2,1)} custom-call(s32[32]{0:T(128)} %bitcast.26, s32[32]{0:T(128)} %bitcast.27, s32[2]{0:T(128)} %pad_add_fusion.1.counts, bf16[8,256,180]{2,1,0:T(8,128)(2,1)} %copy-done.1, bf16[4,256,180]{2,1,0:T(8,128)(2,1)} %bitcast.17, bf16[32,32,180]{2,1,0:T(8,128)(2,1)} %get-tuple-element.12.upper, f32[6,64,64]{2,1,0:T(8,128)} %reshape.97.bias, ...), custom_call_target="tpu_custom_call" | custom-call | flops 10000000000 | bytes 30000000 | tf_op jit(solution)/shard_map/map/pallas_call | solution.py:293
  75.4 2.3 %copy.18 = bf16[8,256,180]{1,0,2:T(8,128)(2,1)} copy(bf16[8,256,180]{2,1,0:T(8,128)(2,1)} %map.1) | data formatting | bytes 1474560
  77.7 0.0 all-to-all-done
  77.7 0.9 %copy-done.2 = bf16[8,384,128]{2,1,0:T(8,128)(2,1)} copy-done((bf16[8,384,128]{2,1,0:T(8,128)(2,1)}, bf16[8,384,128]{2,1,0:T(8,128)(2,1)S(1)}, u32[]{:S(2)}) %copy-start.2) | copy-done | bytes 786456
  78.6 4.6 %place.1 = bf16[8,128,180]{2,1,0:T(8,128)(2,1)} custom-call(bf16[16,192,128]{2,1,0:T(8,128)(2,1)} %bitcast.15), custom_call_target="tpu_custom_call" | custom-call | tf_op jit(solution)/shard_map/place/pallas_call | solution.py:312
  83.3 2.0 %copy.19 = bf16[8,128,180]{1,0,2:T(8,128)(2,1)} copy(bf16[8,128,180]{2,1,0:T(8,128)(2,1)} %place.1) | data formatting | bytes 737280
  (9 shorter events, 0.0 us)
Async XLA Ops:
  0.6 12.6 %copy-start = (f32[225,6]{0,1:T(8,128)S(1)}, f32[225,6]{0,1:T(8,128)}, u32[]{:S(2)}) copy-start(f32[225,6]{0,1:T(8,128)} %param.17) | copy-start | bytes 16204
  2.0 13.3 %collective-permute-start.2 = (s32[33]{0:T(128)S(1)}, s32[33]{0:T(128)S(1)}, u32[]{:S(2)}, u32[]{:S(2)}) collective-permute-start(s32[33]{0:T(128)S(1)} %pad_add_fusion), channel_id=1, source_target_pairs={{0,4},{4,8},{8,12},{12,16},{16,20},{20,24},{24,28},{28,0},{1,5},{5... | collective-permute-start | bytes 404 | tf_op jit(solution)/shard_map/ppermute | solution.py:259
  6.5 1.0 %copy-start.1 = (bf16[8,256,180]{2,1,0:T(8,128)(2,1)}, bf16[8,256,180]{2,1,0:T(8,128)(2,1)S(1)}, u32[]{:S(2)}) copy-start(bf16[8,256,180]{2,1,0:T(8,128)(2,1)S(1)} %copy.14.pixels) | copy-start | bytes 2211844
  6.5 5.9 %copy-start.3 = (bf16[180,540]{1,0:T(8,128)(2,1)S(1)}, bf16[180,540]{1,0:T(8,128)(2,1)}, u32[]{:S(2)}) copy-start(bf16[180,540]{1,0:T(8,128)(2,1)} %param.19) | copy-start | bytes 583204
  7.5 23.7 %collective-permute-start.1 = (bf16[180,4,256]{0,2,1:T(8,128)(2,1)S(1)}, bf16[180,4,256]{0,2,1:T(8,128)(2,1)S(1)}, u32[]{:S(2)}, u32[]{:S(2)}) collective-permute-start(bf16[180,4,256]{0,2,1:T(8,128)(2,1)S(1)} %get-tuple-element.16), channel_id=1, source_target_pairs={{0,4},{4,8},{8,12},{12,16},{16,20},{20,24},{24,28},{28,0},{1,5},{5... | collective-permute-start | bytes 1105928 | tf_op jit(solution)/shard_map/ppermute | solution.py:258
  9.1 24.3 %collective-permute-start = (bf16[180,4,256]{0,2,1:T(8,128)(2,1)S(1)}, bf16[180,4,256]{0,2,1:T(8,128)(2,1)S(1)}, u32[]{:S(2)}, u32[]{:S(2)}) collective-permute-start(bf16[180,4,256]{0,2,1:T(8,128)(2,1)S(1)} %get-tuple-element.17), channel_id=1, source_target_pairs={{0,28},{4,0},{8,4},{12,8},{16,12},{20,16},{24,20},{28,24},{1,29},{... | collective-permute-start | bytes 1105928 | tf_op jit(solution)/shard_map/ppermute | solution.py:257
  15.3 41.1 %copy-start.7 = (s32[33]{0:T(128)}, s32[33]{0:T(128)S(1)}, u32[]{:S(2)}) copy-start(s32[33]{0:T(128)S(1)} %collective-permute-done.2) | copy-start | bytes 400
  31.2 2.2 %copy-start.5 = (bf16[180,4,256]{0,2,1:T(8,128)(2,1)}, bf16[180,4,256]{0,2,1:T(8,128)(2,1)S(1)}, u32[]{:S(2)}) copy-start(bf16[180,4,256]{0,2,1:T(8,128)(2,1)S(1)} %collective-permute-done.1) | copy-start | bytes 1105924
  33.4 0.8 copy-start.6
  51.1 4.5 %copy-start.4 = (bf16[360,180]{0,1:T(8,128)(2,1)S(1)}, bf16[360,180]{0,1:T(8,128)(2,1)}, u32[]{:S(2)}) copy-start(bf16[360,180]{0,1:T(8,128)(2,1)} %param.23) | copy-start | bytes 388804
  51.1 26.6 %all-to-all-start = ((bf16[8,384,128]{2,1,0:T(8,128)(2,1)}), bf16[8,384,128]{2,1,0:T(8,128)(2,1)S(1)}, u32[]{:S(2)}, u32[]{:S(2)}) async-start(bf16[8,384,128]{2,1,0:T(8,128)(2,1)} %bitcast.16), calls=%async_computation | async-start | bytes 1572864 | tf_op jit(solution)/shard_map/all_to_all | solution.py:290
  77.7 0.9 %copy-start.2 = (bf16[8,384,128]{2,1,0:T(8,128)(2,1)}, bf16[8,384,128]{2,1,0:T(8,128)(2,1)S(1)}, u32[]{:S(2)}) copy-start(bf16[8,384,128]{2,1,0:T(8,128)(2,1)S(1)} %all-to-all-done) | copy-start | bytes 2359300

commit v4 on v3

--- a/solution.py
+++ b/solution.py
@@ -111,23 +111,52 @@
 
 
 def own_kernel(
-    keep, count, dests, slots, pixels, nxt, bias, gain_a, wq, wk, wv, wp,
-    upper, outgoing,
-    shifted, first, rest, bias_own, order,
+    pixels, bias, gain_a, wq, wk, wv, wp,
+    upper, first, rest, prv,
+    shifted, nxt_buf, prv_buf, bias_own, send_sem, recv_sem,
 ):
     bands = lax.axis_size("band")
     me = lax.axis_index("band")
-    windows = pixels.shape[1] // WIN
-    tiles = windows // TILE
-    pairs = -(-tiles // bands)
-
-    def scan(w, kept):
-        order[kept] = w
-        return kept + keep[w]
-
-    live = jnp.minimum(lax.fori_loop(0, windows, scan, jnp.int32(0)), count[0])
+    right, left = lax.rem(me + 1, bands), lax.rem(me + bands - 1, bands)
+    rows, cols, _ = pixels.shape
+    windows = cols // WIN
+    groups = windows // GROUP
+    chunks = groups // 2
+    width = cols // chunks
+
+    barrier = pltpu.get_barrier_semaphore()
+    for neighbour in (left, right):
+        pl.semaphore_signal(
+            barrier, inc=1, device_id={"band": neighbour}, device_id_type=pl.DeviceIdType.MESH
+        )
+    pl.semaphore_wait(barrier, 2)
+    copies = []
+    for c in range(chunks):
+        part = pl.ds(c * width, width)
+        copies.append(
+            pltpu.make_async_remote_copy(
+                src_ref=pixels.at[0:SHIFT, part],
+                dst_ref=nxt_buf.at[:, part],
+                send_sem=send_sem.at[c],
+                recv_sem=recv_sem.at[c],
+                device_id={"band": left},
+                device_id_type=pl.DeviceIdType.MESH,
+            )
+        )
+    copies.append(
+        pltpu.make_async_remote_copy(
+            src_ref=pixels.at[rows - SHIFT : rows],
+            dst_ref=prv_buf,
+            send_sem=send_sem.at[chunks],
+            recv_sem=recv_sem.at[chunks],
+            device_id={"band": right},
+            device_id_type=pl.DeviceIdType.MESH,
+        )
+    )
+    for copy in copies:
+        copy.start()
+
     shifted[0 : WIN - SHIFT] = roll_cols(pixels[SHIFT:].astype(F32), SHIFT)
-    shifted[WIN - SHIFT :] = roll_cols(nxt[...].astype(F32), SHIFT)
     bias_own[0], bias_own[1] = biases(bias, me == bands - 1, TOK)
 
     def step(i, _):
@@ -140,10 +169,36 @@
             value = own[g * TOK : (g + 1) * TOK]
             upper[w] = value[:HALF]
             first[w] = value[:, :LANES]
-            rest[w, :, : CHAN - LANES] = value[:, LANES:].astype(F32)
+            rest[w] = value[:, LANES:]
         return 0
 
-    lax.fori_loop(0, windows // GROUP, step, 0)
+    for c in range(chunks):
+        copies[c].wait()
+        low = c * width
+        block = nxt_buf[:, low : low + width].astype(F32)
+        if c == 0:
+            shifted[WIN - SHIFT :, cols - SHIFT :] = block[:, :SHIFT]
+            shifted[WIN - SHIFT :, 0 : width - SHIFT] = block[:, SHIFT:]
+        else:
+            shifted[WIN - SHIFT :, low - SHIFT : low + width - SHIFT] = block
+        begin = 2 * c - 1 if c else 0
+        end = 2 * c + 1 if c < chunks - 1 else groups
+        lax.fori_loop(begin, end, step, 0)
+    copies[chunks].wait()
+    prv[...] = prv_buf[...]
+
+
+def pack_kernel(keep, count, dests, slots, first, rest, outgoing, order):
+    bands = lax.axis_size("band")
+    windows = first.shape[0]
+    tiles = windows // TILE
+    pairs = -(-tiles // bands)
+
+    def scan(w, kept):
+        order[kept] = w
+        return kept + keep[w]
+
+    live = jnp.minimum(lax.fori_loop(0, windows, scan, jnp.int32(0)), count[0])
     if bands * pairs > tiles:
         outgoing[...] = jnp.full(outgoing.shape, CAP, BF)
     lane = lax.broadcasted_iota(jnp.int32, (TOK, LANES), 1)
@@ -158,8 +213,9 @@
             source = jnp.where(valid, order[jnp.where(valid, position, 0)], 0)
             value = first[source]
             outgoing[place, p * TOK : (p + 1) * TOK] = jnp.where(valid, value, jnp.zeros_like(value))
-            tail = rest[source]
-            halves.append(jnp.where(valid & (lane < CHAN - LANES), tail, 0.0))
+            tail = rest[source].astype(F32)
+            tail = jnp.concatenate([tail, jnp.zeros((TOK, 2 * LANES - CHAN), F32)], axis=1)
+            halves.append(jnp.where(valid, tail, 0.0))
         both = jnp.where(lane < TOK, halves[0], pltpu.roll(halves[1], TOK, 1))
         both = jnp.where(lane >= SLOT_LANE, slot, both)
         outgoing[place, TILE * TOK :] = both.astype(BF)
@@ -252,41 +308,49 @@
     tiles = windows // TILE
     pairs = -(-tiles // bands)
     ahead = [(s, (s + 1) % bands) for s in range(bands)]
-    back = [(s, (s - 1) % bands) for s in range(bands)]
-    turned = jnp.transpose(pixels, (2, 0, 1))
-    nxt = jnp.transpose(lax.ppermute(turned[:, :SHIFT], "band", back), (1, 2, 0))
-    prv = jnp.transpose(lax.ppermute(turned[:, rows - SHIFT :], "band", ahead), (1, 2, 0))
     facts = lax.ppermute(jnp.concatenate([keep_mask[0], band_counts]), "band", ahead)
     bias = position_bias(bias_table)
-    nxt, prv, facts, bias = lax.optimization_barrier((nxt, prv, facts, bias))
+    facts, bias = lax.optimization_barrier((facts, bias))
     keep_prev = facts[:windows]
     counts = jnp.concatenate([band_counts, facts[windows:]])
     wq, wk, wv = (qkv_weight[:, i * CHAN : (i + 1) * CHAN] for i in range(3))
     smem = pl.BlockSpec(memory_space=pltpu.SMEM)
     vmem = pl.BlockSpec(memory_space=pltpu.VMEM)
     limit = pltpu.CompilerParams(vmem_limit_bytes=63 * 1024 * 1024)
-    upper, outgoing = pl.pallas_call(
+    chunks = windows // GROUP // 2
+    upper, first, rest, prv = pl.pallas_call(
         own_kernel,
         out_shape=(
             jax.ShapeDtypeStruct((windows, HALF, channels), BF),
-            jax.ShapeDtypeStruct((bands * pairs, TILE * TOK + TOK, LANES), BF),
+            jax.ShapeDtypeStruct((windows, TOK, LANES), BF),
+            jax.ShapeDtypeStruct((windows, TOK, channels - LANES), BF),
+            jax.ShapeDtypeStruct((SHIFT, cols, channels), BF),
         ),
-        in_specs=[smem] * 4 + [vmem] * 8,
-        out_specs=(vmem, vmem),
+        in_specs=[vmem] * 7,
+        out_specs=(vmem,) * 4,
         scratch_shapes=[
             pltpu.VMEM((rows, cols, channels), F32),
-            pltpu.VMEM((windows, TOK, LANES), BF),
-            pltpu.VMEM((windows, TOK, LANES), F32),
+            pltpu.VMEM((SHIFT, cols, channels), BF),
+            pltpu.VMEM((SHIFT, cols, channels), BF),
             pltpu.VMEM((2, HEADS * TOK, TOK), F32),
-            pltpu.SMEM((windows + 1,), jnp.int32),
+            pltpu.SemaphoreType.DMA((chunks + 1,)),
+            pltpu.SemaphoreType.DMA((chunks + 1,)),
         ],
-        compiler_params=limit,
+        compiler_params=pltpu.CompilerParams(
+            vmem_limit_bytes=63 * 1024 * 1024, collective_id=0, has_side_effects=True
+        ),
         cost_estimate=pl.CostEstimate(flops=3 * 10**9, bytes_accessed=10**7, transcendentals=10**6),
         name="own",
-    )(
-        keep_mask[0], band_counts, plan_dest[0], plan_slot[0],
-        pixels, nxt, bias, gain_attn[None], wq, wk, wv, proj_weight,
-    )
+    )(pixels, bias, gain_attn[None], wq, wk, wv, proj_weight)
+    outgoing = pl.pallas_call(
+        pack_kernel,
+        out_shape=jax.ShapeDtypeStruct((bands * pairs, TILE * TOK + TOK, LANES), BF),
+        in_specs=[smem] * 4 + [vmem] * 2,
+        out_specs=vmem,
+        scratch_shapes=[pltpu.SMEM((windows + 1,), jnp.int32)],
+        compiler_params=limit,
+        name="pack",
+    )(keep_mask[0], band_counts, plan_dest[0], plan_slot[0], first, rest)
     incoming = lax.all_to_all(
         outgoing.reshape(bands, -1, LANES), "band", split_axis=0, concat_axis=0, tiled=True
     ).reshape(outgoing.shape)

time: 85.7 us -> 82.3 us (0.960)
  Pallas kernels: 38.7 us -> 60.7 us
  waiting for transfers between devices: 18.1 us -> 0.09 us
  starting transfers between devices: 12.2 us -> 6.64 us
  local copies, waits for them, and re-layouts: 11.7 us -> 9.73 us
    pallas_call x1, Pallas kernels: 16.8 us -> 35.3 us  [shards(): pl.pallas_call(own_kernel, out_shape=(jax.ShapeDtypeStruct((windows, HALF...]
    ppermute x2 -> x0, waiting for transfers between devices: 18.1 us -> none  [the longest x1 15.9 us: shards(): lax.ppermute(turned[:, rows - SHIFT:], 'band', ahead)]
    ppermute x2 -> x0, starting transfers between devices: 4.72 us -> none  [the longest x1 3.17 us: shards(): lax.ppermute(turned[:, :SHIFT], 'band', back)]
    pallas_call x0 -> x1, Pallas kernels: none -> 3.62 us  [shards(): pl.pallas_call(pack_kernel, out_shape=jax.ShapeDtypeStruct((bands * pairs...]
    unnamed x20 -> x16, local copies, waits for them, and re-layouts: 9.31 us -> 7.53 us
  transfers between devices with their start and end apart: 4 -> 2, of which waited for: 2 -> 1; matrix products, arithmetic and copies ran while one was open for 11% -> 11% of each run, Pallas kernels for 20% -> 21%
where the time goes in v4:
time: 82.3 us; the launch traced here: 81.9 us
  Pallas kernels  60.7 us (74%)
  local copies, waits for them, and re-layouts  9.73 us (12%)
  starting transfers between devices  6.64 us (8%)
  other arithmetic  1.94 us (2%)
  between operations  1.43 us (2%)
  matrix products  1.3 us (2%)
    pallas_call x1, Pallas kernels, shards(): pl.pallas_call(own_kernel, out_shape=(jax.ShapeDtypeStruct((windows, HALF...  35.3 us
    pallas_call x1, Pallas kernels, shards(): pl.pallas_call(map_kernel, out_shape=jax.ShapeDtypeStruct((rows, cols, ch...  17.2 us
    unnamed x16, local copies, waits for them, and re-layouts  7.53 us
    pallas_call x1, Pallas kernels, shards(): pl.pallas_call(place_kernel, out_shape=jax.ShapeDtypeStruct((CAP, TILE *...  4.63 us
    all_to_all x1, starting transfers between devices, shards(): lax.all_to_all(outgoing.reshape(bands, -1, LANES), 'band', split_axis=0,...  3.68 us
    pallas_call x1, Pallas kernels, shards(): pl.pallas_call(pack_kernel, out_shape=jax.ShapeDtypeStruct((bands * pairs...  3.62 us
    ppermute x1, starting transfers between devices, shards(): lax.ppermute(jnp.concatenate([keep_mask[0], band_counts]), 'band', ahead)  2.97 us
  transfers between devices with their start and end apart: 2, of which 1 were waited for; matrix products, arithmetic and copies ran while one was open for 11% of the time, Pallas kernels for 21%

profile of v4, /device:TPU:0, one launch (start us, length us, event | category | flops | bytes accessed | tf_op | source)
XLA Modules:
  0.0 81.9 jit_solution(2058504704869054487)
XLA Ops:
  0.6 0.0 copy-start
  0.6 0.0 copy-start.3
  0.7 0.0 copy-start.2
  1.4 0.7 pad_add_fusion
  2.1 3.0 %collective-permute-start = (s32[33]{0:T(128)S(1)}, s32[33]{0:T(128)S(1)}, u32[]{:S(2)}, u32[]{:S(2)}) collective-permute-start(s32[33]{0:T(128)S(1)} %pad_add_fusion), channel_id=1, source_target_pairs={{0,4},{4,8},{8,12},{12,16},{16,20},{20,24},{24,28},{28,0},{1,5},{5... | collective-permute-start | bytes 404 | tf_op jit(solution)/shard_map/ppermute | solution.py:311
  5.1 0.1 add_add_fusion
  5.2 0.1 add.55
  5.3 0.0 copy-done
  5.3 1.3 %convolution_bitcast_fusion = f32[6,4096]{1,0:T(8,128)S(1)} fusion(f32[225,6]{0,1:T(8,128)S(1)} %copy-done, s32[4096]{0:T(1024)S(1)} %add.55), kind=kOutput, calls=%fused_computation | convolution fusion | flops 67276800 | bytes 120088 | tf_op jit(solution)/shard_map/dot_general | solution.py:298
  6.6 0.8 reshape.97.bias
  7.3 0.0 copy-done.3
  7.3 0.8 fusion.1
  8.1 0.0 copy-done.2
  8.1 1.5 %copy.15.pixels = bf16[8,256,180]{2,1,0:T(8,128)(2,1)} copy(bf16[8,256,180]{1,0,2:T(8,128)(2,1)S(1)} %copy-done.2) | data formatting | bytes 1474560 | tf_op args[0]
  9.6 0.1 collective-permute-done
  9.7 0.0 copy-start.5
  9.7 35.3 %own.1 = (bf16[32,32,180]{2,1,0:T(8,128)(2,1)}, bf16[32,64,128]{2,1,0:T(8,128)(2,1)}, bf16[32,64,52]{2,1,0:T(8,128)(2,1)}, bf16[4,256,180]{2,1,0:T(8,128)(2,1)}) custom-call(bf16[8,256,180]{2,1,0:T(8,128)(2,1)} %copy.15.pixels, f32[6,64,64]{2,1,0:T(8,128)} %reshape.97.bias, f32[1,180]{1,0:T(1,128)} %bitcast.18, bf16[180,180]{1,0:T(8,128)(2,1)} %get-tuple-element.17.wq, ...), custom_call_target="tpu_custom_call" | custom-call | flops 3000000000 | bytes 10000000 | tf_op jit(solution)/shard_map/own/pallas_call | solution.py:321
  45.0 3.6 %pack.1 = bf16[16,192,128]{2,1,0:T(8,128)(2,1)} custom-call(s32[32]{0:T(128)} %bitcast.16, s32[1]{0:T(128)S(6)} %copy.19.count, s32[16]{0:T(128)} %bitcast.13, s32[16]{0:T(128)} %bitcast.14, bf16[32,64,128]{2,1,0:T(8,128)(2,1)} %get-tuple-element.12.first, bf16[32,64,52]{2,1,0:T(8,128)(2,1)} %get-tuple-element.13.rest), custom_call_target="tpu_custom_call" | custom-call | tf_op jit(solution)/shard_map/pack/pallas_call | solution.py:345
  48.6 0.0 copy-start.4
  48.6 3.7 %all-to-all-start = ((bf16[8,384,128]{2,1,0:T(8,128)(2,1)}), bf16[8,384,128]{2,1,0:T(8,128)(2,1)S(1)}, u32[]{:S(2)}, u32[]{:S(2)}) async-start(bf16[8,384,128]{2,1,0:T(8,128)(2,1)} %bitcast.12), calls=%async_computation | async-start | bytes 1572864 | tf_op jit(solution)/shard_map/all_to_all | solution.py:354
  52.3 0.0 copy-done.4
  52.3 0.8 copy.16.wo
  53.1 0.0 copy-done.5
  53.1 0.6 slice.16
  53.7 1.1 %pad_add_fusion.1.counts = s32[2]{0:T(128)} fusion(s32[1]{0:T(128)} %slice.16, s32[1]{0:T(128)S(6)} %copy.19.count), kind=kLoop, calls=%fused_computation.10 | loop fusion | flops 2 | bytes 16 | tf_op jit(solution)/shard_map/concatenate | solution.py:315
  54.8 17.2 %map.1 = bf16[8,256,180]{2,1,0:T(8,128)(2,1)} custom-call(s32[32]{0:T(128)} %bitcast.17, s32[32]{0:T(128)} %bitcast.21, s32[2]{0:T(128)} %pad_add_fusion.1.counts, bf16[8,256,180]{2,1,0:T(8,128)(2,1)} %copy.15.pixels, bf16[4,256,180]{2,1,0:T(8,128)(2,1)} %get-tuple-element.10.prv, bf16[32,32,180]{2,1,0:T(8,128)(2,1)} %get-tuple-element.11.upper, ...), custom_call_target="tpu_custom_call" | custom-call | flops 10000000000 | bytes 30000000 | tf_op jit(solution)/shard_map/map/pallas_call | solution.py:357
  72.0 2.3 %copy.17 = bf16[8,256,180]{1,0,2:T(8,128)(2,1)} copy(bf16[8,256,180]{2,1,0:T(8,128)(2,1)} %map.1) | data formatting | bytes 1474560
  74.3 0.0 all-to-all-done
  74.3 0.0 copy-start.1
  74.3 0.9 %copy-done.1 = bf16[8,384,128]{2,1,0:T(8,128)(2,1)} copy-done((bf16[8,384,128]{2,1,0:T(8,128)(2,1)}, bf16[8,384,128]{2,1,0:T(8,128)(2,1)S(1)}, u32[]{:S(2)}) %copy-start.1) | copy-done | bytes 786456
  75.2 4.6 %place.1 = bf16[8,128,180]{2,1,0:T(8,128)(2,1)} custom-call(bf16[16,192,128]{2,1,0:T(8,128)(2,1)} %bitcast.11), custom_call_target="tpu_custom_call" | custom-call | tf_op jit(solution)/shard_map/place/pallas_call | solution.py:376
  79.8 2.0 %copy.18 = bf16[8,128,180]{1,0,2:T(8,128)(2,1)} copy(bf16[8,128,180]{2,1,0:T(8,128)(2,1)} %place.1) | data formatting | bytes 737280
  (1 shorter events, 0.0 us)
Async XLA Ops:
  0.6 4.6 %copy-start = (f32[225,6]{0,1:T(8,128)S(1)}, f32[225,6]{0,1:T(8,128)}, u32[]{:S(2)}) copy-start(f32[225,6]{0,1:T(8,128)} %param.17) | copy-start | bytes 16204
  0.6 6.7 %copy-start.3 = (bf16[180,540]{1,0:T(8,128)(2,1)S(1)}, bf16[180,540]{1,0:T(8,128)(2,1)}, u32[]{:S(2)}) copy-start(bf16[180,540]{1,0:T(8,128)(2,1)} %param.19) | copy-start | bytes 583204
  0.7 7.5 %copy-start.2 = (bf16[8,256,180]{1,0,2:T(8,128)(2,1)S(1)}, bf16[8,256,180]{1,0,2:T(8,128)(2,1)}, u32[]{:S(2)}) copy-start(bf16[8,256,180]{1,0,2:T(8,128)(2,1)} %param.12) | copy-start | bytes 2211844
  2.1 7.6 %collective-permute-start = (s32[33]{0:T(128)S(1)}, s32[33]{0:T(128)S(1)}, u32[]{:S(2)}, u32[]{:S(2)}) collective-permute-start(s32[33]{0:T(128)S(1)} %pad_add_fusion), channel_id=1, source_target_pairs={{0,4},{4,8},{8,12},{12,16},{16,20},{20,24},{24,28},{28,0},{1,5},{5... | collective-permute-start | bytes 404 | tf_op jit(solution)/shard_map/ppermute | solution.py:311
  9.7 43.4 %copy-start.5 = (s32[33]{0:T(128)}, s32[33]{0:T(128)S(1)}, u32[]{:S(2)}) copy-start(s32[33]{0:T(128)S(1)} %collective-permute-done) | copy-start | bytes 400
  48.6 3.7 %copy-start.4 = (bf16[360,180]{0,1:T(8,128)(2,1)S(1)}, bf16[360,180]{0,1:T(8,128)(2,1)}, u32[]{:S(2)}) copy-start(bf16[360,180]{0,1:T(8,128)(2,1)} %param.23) | copy-start | bytes 388804
  48.6 25.7 %all-to-all-start = ((bf16[8,384,128]{2,1,0:T(8,128)(2,1)}), bf16[8,384,128]{2,1,0:T(8,128)(2,1)S(1)}, u32[]{:S(2)}, u32[]{:S(2)}) async-start(bf16[8,384,128]{2,1,0:T(8,128)(2,1)} %bitcast.12), calls=%async_computation | async-start | bytes 1572864 | tf_op jit(solution)/shard_map/all_to_all | solution.py:354
  74.3 0.9 %copy-start.1 = (bf16[8,384,128]{2,1,0:T(8,128)(2,1)}, bf16[8,384,128]{2,1,0:T(8,128)(2,1)S(1)}, u32[]{:S(2)}) copy-start(bf16[8,384,128]{2,1,0:T(8,128)(2,1)S(1)} %all-to-all-done) | copy-start | bytes 2359300

commit v5 on v4

--- a/solution.py
+++ b/solution.py
@@ -93,7 +93,7 @@
     flat = states.astype(F32)
     normed = layer_norm(flat, gain)
     inner = jax.nn.gelu(dot(normed, wh)).astype(BF)
-    return (flat + dot(inner, wo)).astype(BF)
+    return (flat + dot_t(inner, wo)).astype(BF)
 
 
 def roll_cols(x, by):
@@ -153,7 +153,7 @@
             device_id_type=pl.DeviceIdType.MESH,
         )
     )
-    for copy in copies:
+    for copy in copies[:chunks]:
         copy.start()
 
     shifted[0 : WIN - SHIFT] = roll_cols(pixels[SHIFT:].astype(F32), SHIFT)
@@ -174,6 +174,8 @@
 
     for c in range(chunks):
         copies[c].wait()
+        if c == chunks // 2:
+            copies[chunks].start()
         low = c * width
         block = nxt_buf[:, low : low + width].astype(F32)
         if c == 0:
@@ -225,7 +227,7 @@
 
 
 def map_kernel(
-    keep_own, keep_prev, counts, pixels, prv, upper, bias, gain_a, wq, wk, wv, wp, gain_m, wh, wo,
+    keep_own, count, facts, pixels, prv, upper, bias, gain_a, wq, wk, wv, wp, gain_m, wh, wo,
     restored,
     shifted, result, bias_prev, act_own, act_prev,
 ):
@@ -234,9 +236,9 @@
 
     def scan(w, carry):
         own, prev = carry
-        act_own[w] = ((keep_own[w] == 1) & (own < counts[0])).astype(jnp.int32)
-        act_prev[w] = ((keep_prev[w] == 1) & (prev < counts[1])).astype(jnp.int32)
-        return own + keep_own[w], prev + keep_prev[w]
+        act_own[w] = ((keep_own[w] == 1) & (own < count[0])).astype(jnp.int32)
+        act_prev[w] = ((facts[w] == 1) & (prev < facts[windows])).astype(jnp.int32)
+        return own + keep_own[w], prev + facts[w]
 
     lax.fori_loop(0, windows, scan, (jnp.int32(0), jnp.int32(0)))
     shifted[0:SHIFT] = roll_cols(prv[...].astype(F32), SHIFT)
@@ -311,8 +313,6 @@
     facts = lax.ppermute(jnp.concatenate([keep_mask[0], band_counts]), "band", ahead)
     bias = position_bias(bias_table)
     facts, bias = lax.optimization_barrier((facts, bias))
-    keep_prev = facts[:windows]
-    counts = jnp.concatenate([band_counts, facts[windows:]])
     wq, wk, wv = (qkv_weight[:, i * CHAN : (i + 1) * CHAN] for i in range(3))
     smem = pl.BlockSpec(memory_space=pltpu.SMEM)
     vmem = pl.BlockSpec(memory_space=pltpu.VMEM)
@@ -370,15 +370,15 @@
         cost_estimate=pl.CostEstimate(flops=10**10, bytes_accessed=3 * 10**7, transcendentals=10**6),
         name="map",
     )(
-        keep_mask[0], keep_prev, counts, pixels, prv, upper, bias, gain_attn[None], wq, wk, wv,
-        proj_weight, gain_mlp[None], hidden_weight, output_weight,
+        keep_mask[0], band_counts, facts, pixels, prv, upper, bias, gain_attn[None], wq, wk, wv,
+        proj_weight, gain_mlp[None], hidden_weight, output_weight.T,
     )
     work = pl.pallas_call(
         place_kernel,
         out_shape=jax.ShapeDtypeStruct((CAP, TILE * TOK, channels), BF),
         in_specs=[vmem],
         out_specs=vmem,
-        compiler_params=limit,
+        compiler_params=pltpu.CompilerParams(vmem_limit_bytes=16 * 1024 * 1024),
         name="place",
     )(incoming)
     return restored, work

time: 82.3 us -> 74.1 us (0.900)
  Pallas kernels: 60.7 us -> 54.5 us
  local copies, waits for them, and re-layouts: 9.73 us -> 6.41 us
  starting transfers between devices: 6.64 us -> 9.19 us
  other arithmetic: 1.94 us -> 0.82 us
    pallas_call x1, Pallas kernels: 35.3 us -> 30.8 us  [shards(): pl.pallas_call(own_kernel, out_shape=(jax.ShapeDtypeStruct((windows, HALF...]
    unnamed x16 -> x11, local copies, waits for them, and re-layouts: 7.53 us -> 4.78 us
    all_to_all x1, starting transfers between devices: 3.68 us -> 6.22 us  [shards(): lax.all_to_all(outgoing.reshape(bands, -1, LANES), 'band', split_axis=0,...]
    pallas_call x1, Pallas kernels: 4.63 us -> 2.68 us  [shards(): pl.pallas_call(place_kernel, out_shape=jax.ShapeDtypeStruct((CAP, TILE *...]
    concatenate x1 -> x0, other arithmetic: 1.12 us -> none  [shards(): counts = jnp.concatenate([band_counts, facts[windows:]])]
  transfers between devices with their start and end apart: 2 -> 2, of which waited for: 1 -> 1; matrix products, arithmetic and copies ran while one was open for 11% -> 9% of each run, Pallas kernels for 21% -> 24%
where the time goes in v5:
time: 74.1 us; the launch traced here: 73.8 us
  Pallas kernels  54.5 us (74%)
  starting transfers between devices  9.19 us (12%)
  local copies, waits for them, and re-layouts  6.41 us (9%)
  between operations  1.42 us (2%)
  matrix products  1.3 us (2%)
  other arithmetic  0.82 us (1%)
    pallas_call x1, Pallas kernels, shards(): pl.pallas_call(own_kernel, out_shape=(jax.ShapeDtypeStruct((windows, HALF...  30.8 us
    pallas_call x1, Pallas kernels, shards(): pl.pallas_call(map_kernel, out_shape=jax.ShapeDtypeStruct((rows, cols, ch...  17.5 us
    all_to_all x1, starting transfers between devices, shards(): lax.all_to_all(outgoing.reshape(bands, -1, LANES), 'band', split_axis=0,...  6.22 us
    unnamed x11, local copies, waits for them, and re-layouts  4.78 us
    pallas_call x1, Pallas kernels, shards(): pl.pallas_call(pack_kernel, out_shape=jax.ShapeDtypeStruct((bands * pairs...  3.62 us
    ppermute x1, starting transfers between devices, shards(): lax.ppermute(jnp.concatenate([keep_mask[0], band_counts]), 'band', ahead)  2.97 us
    pallas_call x1, Pallas kernels, shards(): pl.pallas_call(place_kernel, out_shape=jax.ShapeDtypeStruct((CAP, TILE *...  2.68 us
  transfers between devices with their start and end apart: 2, of which 1 were waited for; matrix products, arithmetic and copies ran while one was open for 9% of the time, Pallas kernels for 24%

profile of v5, /device:TPU:0, one launch (start us, length us, event | category | flops | bytes accessed | tf_op | source)
XLA Modules:
  0.0 73.8 jit_solution(11047477540327173123)
XLA Ops:
  0.6 0.0 copy-start
  0.6 0.0 copy-start.2
  0.7 0.0 copy-start.1
  1.4 0.7 pad_add_fusion
  2.1 3.0 %collective-permute-start = (s32[33]{0:T(128)S(1)}, s32[33]{0:T(128)S(1)}, u32[]{:S(2)}, u32[]{:S(2)}) collective-permute-start(s32[33]{0:T(128)S(1)} %pad_add_fusion), channel_id=1, source_target_pairs={{0,4},{4,8},{8,12},{12,16},{16,20},{20,24},{24,28},{28,0},{1,5},{5... | collective-permute-start | bytes 404 | tf_op jit(solution)/shard_map/ppermute | solution.py:313
  5.1 0.1 add_add_fusion
  5.2 0.1 add.55
  5.3 0.0 copy-done
  5.3 1.3 %convolution_bitcast_fusion = f32[6,4096]{1,0:T(8,128)S(1)} fusion(f32[225,6]{0,1:T(8,128)S(1)} %copy-done, s32[4096]{0:T(1024)S(1)} %add.55), kind=kOutput, calls=%fused_computation | convolution fusion | flops 67276800 | bytes 120088 | tf_op jit(solution)/shard_map/dot_general | solution.py:300
  6.6 0.8 %reshape.97.bias = f32[6,64,64]{2,1,0:T(8,128)} reshape(f32[6,4096]{1,0:T(8,128)S(1)} %convolution_bitcast_fusion) | data formatting | bytes 196608 | tf_op jit(solution)/shard_map/reshape | solution.py:300
  7.3 0.0 copy-done.2
  7.3 0.8 %fusion.1 = (bf16[180,180]{1,0:T(8,128)(2,1)}, bf16[180,180]{1,0:T(8,128)(2,1)}, bf16[180,180]{1,0:T(8,128)(2,1)}) fusion(bf16[180,540]{1,0:T(8,128)(2,1)S(1)} %copy-done.2), kind=kLoop, calls=%fused_computation.10 | loop fusion | bytes 388800 | tf_op jit(solution)/shard_map/slice | solution.py:316
  8.1 0.0 copy-done.1
  8.1 1.5 %copy.15.pixels = bf16[8,256,180]{2,1,0:T(8,128)(2,1)} copy(bf16[8,256,180]{1,0,2:T(8,128)(2,1)S(1)} %copy-done.1) | data formatting | bytes 1474560 | tf_op args[0]
  9.6 0.1 collective-permute-done.facts
  9.7 0.0 copy-start.3
  9.7 30.8 %own.1 = (bf16[32,32,180]{2,1,0:T(8,128)(2,1)}, bf16[32,64,128]{2,1,0:T(8,128)(2,1)}, bf16[32,64,52]{2,1,0:T(8,128)(2,1)}, bf16[4,256,180]{2,1,0:T(8,128)(2,1)}) custom-call(bf16[8,256,180]{2,1,0:T(8,128)(2,1)} %copy.15.pixels, f32[6,64,64]{2,1,0:T(8,128)} %reshape.97.bias, f32[1,180]{1,0:T(1,128)} %bitcast.19, bf16[180,180]{1,0:T(8,128)(2,1)} %get-tuple-element.17.wq, ...), custom_call_target="tpu_custom_call" | custom-call | flops 3000000000 | bytes 10000000 | tf_op jit(solution)/shard_map/own/pallas_call | solution.py:321
  40.5 0.0 copy-done.3
  40.5 3.6 %pack.1 = bf16[16,192,128]{2,1,0:T(8,128)(2,1)} custom-call(s32[32]{0:T(128)} %bitcast.16, s32[1]{0:T(128)S(6)} %copy.18.count, s32[16]{0:T(128)} %bitcast.13, s32[16]{0:T(128)} %bitcast.14, bf16[32,64,128]{2,1,0:T(8,128)(2,1)} %get-tuple-element.12.first, bf16[32,64,52]{2,1,0:T(8,128)(2,1)} %get-tuple-element.13.rest), custom_call_target="tpu_custom_call" | custom-call | tf_op jit(solution)/shard_map/pack/pallas_call | solution.py:345
  44.1 6.2 %all-to-all-start = ((bf16[8,384,128]{2,1,0:T(8,128)(2,1)}), bf16[8,384,128]{2,1,0:T(8,128)(2,1)S(1)}, u32[]{:S(2)}, u32[]{:S(2)}) async-start(bf16[8,384,128]{2,1,0:T(8,128)(2,1)} %bitcast.12), calls=%async_computation | async-start | bytes 1572864 | tf_op jit(solution)/shard_map/all_to_all | solution.py:354
  50.3 17.5 %map.1 = bf16[8,256,180]{2,1,0:T(8,128)(2,1)} custom-call(s32[32]{0:T(128)} %bitcast.17, s32[1]{0:T(128)S(6)} %copy.18.count, s32[33]{0:T(128)} %copy-done.3, bf16[8,256,180]{2,1,0:T(8,128)(2,1)} %copy.15.pixels, bf16[4,256,180]{2,1,0:T(8,128)(2,1)} %get-tuple-element.10.prv, bf16[32,32,180]{2,1,0:T(8,128)(2,1)} %get-tuple-element.11.upper, ...), custom_call_target="tpu_custom_call" | custom-call | flops 10000000000 | bytes 30000000 | tf_op jit(solution)/shard_map/map/pallas_call | solution.py:357
  67.8 2.3 %copy.16 = bf16[8,256,180]{1,0,2:T(8,128)(2,1)} copy(bf16[8,256,180]{2,1,0:T(8,128)(2,1)} %map.1) | data formatting | bytes 1474560
  70.1 0.0 all-to-all-done
  70.1 2.7 %place.1 = bf16[8,128,180]{2,1,0:T(8,128)(2,1)S(1)} custom-call(bf16[16,192,128]{2,1,0:T(8,128)(2,1)S(1)} %bitcast.11), custom_call_target="tpu_custom_call" | custom-call | tf_op jit(solution)/shard_map/place/pallas_call | solution.py:376
  72.8 1.0 %copy.17 = bf16[8,128,180]{1,0,2:T(8,128)(2,1)} copy(bf16[8,128,180]{2,1,0:T(8,128)(2,1)S(1)} %place.1) | data formatting | bytes 737280
  (1 shorter events, 0.0 us)
Async XLA Ops:
  0.6 4.6 %copy-start = (f32[225,6]{0,1:T(8,128)S(1)}, f32[225,6]{0,1:T(8,128)}, u32[]{:S(2)}) copy-start(f32[225,6]{0,1:T(8,128)} %param.17) | copy-start | bytes 16204
  0.6 6.7 %copy-start.2 = (bf16[180,540]{1,0:T(8,128)(2,1)S(1)}, bf16[180,540]{1,0:T(8,128)(2,1)}, u32[]{:S(2)}) copy-start(bf16[180,540]{1,0:T(8,128)(2,1)} %param.19) | copy-start | bytes 583204
  0.7 7.5 %copy-start.1 = (bf16[8,256,180]{1,0,2:T(8,128)(2,1)S(1)}, bf16[8,256,180]{1,0,2:T(8,128)(2,1)}, u32[]{:S(2)}) copy-start(bf16[8,256,180]{1,0,2:T(8,128)(2,1)} %param.12) | copy-start | bytes 2211844
  2.1 7.6 %collective-permute-start = (s32[33]{0:T(128)S(1)}, s32[33]{0:T(128)S(1)}, u32[]{:S(2)}, u32[]{:S(2)}) collective-permute-start(s32[33]{0:T(128)S(1)} %pad_add_fusion), channel_id=1, source_target_pairs={{0,4},{4,8},{8,12},{12,16},{16,20},{20,24},{24,28},{28,0},{1,5},{5... | collective-permute-start | bytes 404 | tf_op jit(solution)/shard_map/ppermute | solution.py:313
  9.7 30.8 %copy-start.3 = (s32[33]{0:T(128)}, s32[33]{0:T(128)S(1)}, u32[]{:S(2)}) copy-start(s32[33]{0:T(128)S(1)} %collective-permute-done.facts) | copy-start | bytes 400
  44.1 26.0 %all-to-all-start = ((bf16[8,384,128]{2,1,0:T(8,128)(2,1)}), bf16[8,384,128]{2,1,0:T(8,128)(2,1)S(1)}, u32[]{:S(2)}, u32[]{:S(2)}) async-start(bf16[8,384,128]{2,1,0:T(8,128)(2,1)} %bitcast.12), calls=%async_computation | async-start | bytes 1572864 | tf_op jit(solution)/shard_map/all_to_all | solution.py:354

commit v6 on v5

--- a/solution.py
+++ b/solution.py
@@ -111,9 +111,9 @@
 
 
 def own_kernel(
-    pixels, bias, gain_a, wq, wk, wv, wp,
-    upper, first, rest, prv,
-    shifted, nxt_buf, prv_buf, bias_own, send_sem, recv_sem,
+    pixels, told, bias, gain_a, wq, wk, wv, wp,
+    upper, first, rest, prv, facts,
+    shifted, nxt_buf, prv_buf, facts_buf, bias_own, send_sem, recv_sem,
 ):
     bands = lax.axis_size("band")
     me = lax.axis_index("band")
@@ -153,8 +153,19 @@
             device_id_type=pl.DeviceIdType.MESH,
         )
     )
+    copies.append(
+        pltpu.make_async_remote_copy(
+            src_ref=told,
+            dst_ref=facts_buf,
+            send_sem=send_sem.at[chunks + 1],
+            recv_sem=recv_sem.at[chunks + 1],
+            device_id={"band": right},
+            device_id_type=pl.DeviceIdType.MESH,
+        )
+    )
     for copy in copies[:chunks]:
         copy.start()
+    copies[chunks + 1].start()
 
     shifted[0 : WIN - SHIFT] = roll_cols(pixels[SHIFT:].astype(F32), SHIFT)
     bias_own[0], bias_own[1] = biases(bias, me == bands - 1, TOK)
@@ -186,6 +197,8 @@
         begin = 2 * c - 1 if c else 0
         end = 2 * c + 1 if c < chunks - 1 else groups
         lax.fori_loop(begin, end, step, 0)
+    copies[chunks + 1].wait()
+    facts[...] = facts_buf[...]
     copies[chunks].wait()
     prv[...] = prv_buf[...]
 
@@ -237,8 +250,8 @@
     def scan(w, carry):
         own, prev = carry
         act_own[w] = ((keep_own[w] == 1) & (own < count[0])).astype(jnp.int32)
-        act_prev[w] = ((facts[w] == 1) & (prev < facts[windows])).astype(jnp.int32)
-        return own + keep_own[w], prev + facts[w]
+        act_prev[w] = ((facts[0, w] == 1) & (prev < facts[0, windows])).astype(jnp.int32)
+        return own + keep_own[w], prev + facts[0, w]
 
     lax.fori_loop(0, windows, scan, (jnp.int32(0), jnp.int32(0)))
     shifted[0:SHIFT] = roll_cols(prv[...].astype(F32), SHIFT)
@@ -309,39 +322,40 @@
     windows = cols // WIN
     tiles = windows // TILE
     pairs = -(-tiles // bands)
-    ahead = [(s, (s + 1) % bands) for s in range(bands)]
-    facts = lax.ppermute(jnp.concatenate([keep_mask[0], band_counts]), "band", ahead)
+    told = jnp.concatenate([keep_mask[0], band_counts])
+    told = jnp.pad(told, (0, -told.shape[0] % LANES))[None]
     bias = position_bias(bias_table)
-    facts, bias = lax.optimization_barrier((facts, bias))
     wq, wk, wv = (qkv_weight[:, i * CHAN : (i + 1) * CHAN] for i in range(3))
     smem = pl.BlockSpec(memory_space=pltpu.SMEM)
     vmem = pl.BlockSpec(memory_space=pltpu.VMEM)
     limit = pltpu.CompilerParams(vmem_limit_bytes=63 * 1024 * 1024)
     chunks = windows // GROUP // 2
-    upper, first, rest, prv = pl.pallas_call(
+    upper, first, rest, prv, facts = pl.pallas_call(
         own_kernel,
         out_shape=(
             jax.ShapeDtypeStruct((windows, HALF, channels), BF),
             jax.ShapeDtypeStruct((windows, TOK, LANES), BF),
             jax.ShapeDtypeStruct((windows, TOK, channels - LANES), BF),
             jax.ShapeDtypeStruct((SHIFT, cols, channels), BF),
+            jax.ShapeDtypeStruct(told.shape, jnp.int32),
         ),
-        in_specs=[vmem] * 7,
-        out_specs=(vmem,) * 4,
+        in_specs=[vmem] * 8,
+        out_specs=(vmem,) * 5,
         scratch_shapes=[
             pltpu.VMEM((rows, cols, channels), F32),
             pltpu.VMEM((SHIFT, cols, channels), BF),
             pltpu.VMEM((SHIFT, cols, channels), BF),
+            pltpu.VMEM(told.shape, jnp.int32),
             pltpu.VMEM((2, HEADS * TOK, TOK), F32),
-            pltpu.SemaphoreType.DMA((chunks + 1,)),
-            pltpu.SemaphoreType.DMA((chunks + 1,)),
+            pltpu.SemaphoreType.DMA((chunks + 2,)),
+            pltpu.SemaphoreType.DMA((chunks + 2,)),
         ],
         compiler_params=pltpu.CompilerParams(
             vmem_limit_bytes=63 * 1024 * 1024, collective_id=0, has_side_effects=True
         ),
         cost_estimate=pl.CostEstimate(flops=3 * 10**9, bytes_accessed=10**7, transcendentals=10**6),
         name="own",
-    )(pixels, bias, gain_attn[None], wq, wk, wv, proj_weight)
+    )(pixels, told, bias, gain_attn[None], wq, wk, wv, proj_weight)
     outgoing = pl.pallas_call(
         pack_kernel,
         out_shape=jax.ShapeDtypeStruct((bands * pairs, TILE * TOK + TOK, LANES), BF),

time: 74.1 us -> 73.5 us (level)
  starting transfers between devices: 9.19 us -> 5.03 us
  Pallas kernels: 54.5 us -> 57.5 us
    pallas_call x1, Pallas kernels: 30.8 us -> 33.8 us  [shards(): pl.pallas_call(own_kernel, out_shape=(jax.ShapeDtypeStruct((windows, HALF...]
    ppermute x1 -> x0, starting transfers between devices: 2.97 us -> none  [shards(): lax.ppermute(jnp.concatenate([keep_mask[0], band_counts]), 'band', ahead)]
    all_to_all x1, starting transfers between devices: 6.22 us -> 5.03 us  [shards(): lax.all_to_all(outgoing.reshape(bands, -1, LANES), 'band', split_axis=0,...]
    unnamed x11 -> x9, local copies, waits for them, and re-layouts: 4.78 us -> 4.81 us
  transfers between devices with their start and end apart: 2 -> 1, of which waited for: 1 -> 0; matrix products, arithmetic and copies ran while one was open for 9% -> 3% of each run, Pallas kernels for 24% -> 24%
where the time goes in v6:
time: 73.5 us; the launch traced here: 73.1 us
  Pallas kernels  57.5 us (78%)
  local copies, waits for them, and re-layouts  7.03 us (10%)
  starting transfers between devices  5.03 us (7%)
  between operations  1.41 us (2%)
  matrix products  1.3 us (2%)
  other arithmetic  0.81 us (1%)
    pallas_call x1, Pallas kernels, shards(): pl.pallas_call(own_kernel, out_shape=(jax.ShapeDtypeStruct((windows, HALF...  33.8 us
    pallas_call x1, Pallas kernels, shards(): pl.pallas_call(map_kernel, out_shape=jax.ShapeDtypeStruct((rows, cols, ch...  17.5 us
    all_to_all x1, starting transfers between devices, shards(): lax.all_to_all(outgoing.reshape(bands, -1, LANES), 'band', split_axis=0,...  5.03 us
    unnamed x9, local copies, waits for them, and re-layouts  4.81 us
    pallas_call x1, Pallas kernels, shards(): pl.pallas_call(pack_kernel, out_shape=jax.ShapeDtypeStruct((bands * pairs...  3.61 us
    pallas_call x1, Pallas kernels, shards(): pl.pallas_call(place_kernel, out_shape=jax.ShapeDtypeStruct((CAP, TILE *...  2.68 us
  transfers between devices with their start and end apart: 1, of which 0 were waited for; matrix products, arithmetic and copies ran while one was open for 3% of the time, Pallas kernels for 24%

profile of v6, /device:TPU:0, one launch (start us, length us, event | category | flops | bytes accessed | tf_op | source)
XLA Modules:
  0.0 73.1 jit_solution(2091677623498159824)
XLA Ops:
  0.6 0.0 copy-start
  0.6 0.0 copy-start.2
  0.7 0.0 copy-start.1
  1.4 0.7 pad_add_fusion
  2.1 0.6 pad_bitcast_fusion.told
  2.7 0.1 add_add_fusion
  2.8 0.1 add.57
  2.9 0.0 copy-done
  2.9 1.3 %convolution_bitcast_fusion = f32[6,4096]{1,0:T(8,128)S(1)} fusion(f32[225,6]{0,1:T(8,128)S(1)} %copy-done, s32[4096]{0:T(1024)S(1)} %add.57), kind=kOutput, calls=%fused_computation | convolution fusion | flops 67276800 | bytes 120088 | tf_op jit(solution)/shard_map/dot_general | solution.py:313
  4.2 0.8 %reshape.97.bias = f32[6,64,64]{2,1,0:T(8,128)} reshape(f32[6,4096]{1,0:T(8,128)S(1)} %convolution_bitcast_fusion) | data formatting | bytes 196608 | tf_op jit(solution)/shard_map/reshape | solution.py:313
  5.0 0.0 copy-done.2
  5.0 0.8 %fusion.1 = (bf16[180,180]{1,0:T(8,128)(2,1)}, bf16[180,180]{1,0:T(8,128)(2,1)}, bf16[180,180]{1,0:T(8,128)(2,1)}) fusion(bf16[180,540]{1,0:T(8,128)(2,1)S(1)} %copy-done.2), kind=kLoop, calls=%fused_computation.11 | loop fusion | bytes 388800 | tf_op jit(solution)/shard_map/slice | solution.py:328
  5.8 0.0 copy-done.1
  5.8 1.5 %copy.14.pixels = bf16[8,256,180]{2,1,0:T(8,128)(2,1)} copy(bf16[8,256,180]{1,0,2:T(8,128)(2,1)S(1)} %copy-done.1) | data formatting | bytes 1474560 | tf_op args[0]
  7.2 33.8 %own.1 = (bf16[32,32,180]{2,1,0:T(8,128)(2,1)}, bf16[32,64,128]{2,1,0:T(8,128)(2,1)}, bf16[32,64,52]{2,1,0:T(8,128)(2,1)}, bf16[4,256,180]{2,1,0:T(8,128)(2,1)}, s32[1,128]{1,0:T(1,128)}) custom-call(bf16[8,256,180]{2,1,0:T(8,128)(2,1)} %copy.14.pixels, s32[1,128]{1,0:T(1,128)} %pad_bitcast_fusion.told, f32[6,64,64]{2,1,0:T(8,128)} %reshape.97.bias, ...), custom_call_target="tpu_custom_call" | custom-call | flops 3000000000 | bytes 10000000 | tf_op jit(solution)/shard_map/own/pallas_call | solution.py:333
  41.0 3.6 %pack.1 = bf16[16,192,128]{2,1,0:T(8,128)(2,1)} custom-call(s32[32]{0:T(128)} %bitcast.18, s32[1]{0:T(128)S(6)} %copy.18.count, s32[16]{0:T(128)} %bitcast.15, s32[16]{0:T(128)} %bitcast.16, bf16[32,64,128]{2,1,0:T(8,128)(2,1)} %get-tuple-element.10.first, bf16[32,64,52]{2,1,0:T(8,128)(2,1)} %get-tuple-element.11.rest), custom_call_target="tpu_custom_call" | custom-call | tf_op jit(solution)/shard_map/pack/pallas_call | solution.py:359
  44.6 5.0 %all-to-all-start = ((bf16[8,384,128]{2,1,0:T(8,128)(2,1)}), bf16[8,384,128]{2,1,0:T(8,128)(2,1)S(1)}, u32[]{:S(2)}, u32[]{:S(2)}) async-start(bf16[8,384,128]{2,1,0:T(8,128)(2,1)} %bitcast.14), calls=%async_computation | async-start | bytes 1572864 | tf_op jit(solution)/shard_map/all_to_all | solution.py:368
  49.7 17.5 %map.1 = bf16[8,256,180]{2,1,0:T(8,128)(2,1)} custom-call(s32[32]{0:T(128)} %bitcast.19, s32[1]{0:T(128)S(6)} %copy.18.count, s32[1,128]{1,0:T(1,128)} %get-tuple-element.7.facts, bf16[8,256,180]{2,1,0:T(8,128)(2,1)} %copy.14.pixels, bf16[4,256,180]{2,1,0:T(8,128)(2,1)} %get-tuple-element.8.prv, bf16[32,32,180]{2,1,0:T(8,128)(2,1)} %get-tuple-element.9.upper, ...), custom_call_target="tpu_custom_call" | custom-call | flops 10000000000 | bytes 30000000 | tf_op jit(solution)/shard_map/map/pallas_call | solution.py:371
  67.1 2.3 %copy.16 = bf16[8,256,180]{1,0,2:T(8,128)(2,1)} copy(bf16[8,256,180]{2,1,0:T(8,128)(2,1)} %map.1) | data formatting | bytes 1474560
  69.4 0.0 all-to-all-done
  69.5 2.7 %place.1 = bf16[8,128,180]{2,1,0:T(8,128)(2,1)S(1)} custom-call(bf16[16,192,128]{2,1,0:T(8,128)(2,1)S(1)} %bitcast.13), custom_call_target="tpu_custom_call" | custom-call | tf_op jit(solution)/shard_map/place/pallas_call | solution.py:390
  72.1 1.0 %copy.17 = bf16[8,128,180]{1,0,2:T(8,128)(2,1)} copy(bf16[8,128,180]{2,1,0:T(8,128)(2,1)S(1)} %place.1) | data formatting | bytes 737280
  (1 shorter events, 0.0 us)
Async XLA Ops:
  0.6 2.2 %copy-start = (f32[225,6]{0,1:T(8,128)S(1)}, f32[225,6]{0,1:T(8,128)}, u32[]{:S(2)}) copy-start(f32[225,6]{0,1:T(8,128)} %param.17) | copy-start | bytes 16204
  0.6 4.3 %copy-start.2 = (bf16[180,540]{1,0:T(8,128)(2,1)S(1)}, bf16[180,540]{1,0:T(8,128)(2,1)}, u32[]{:S(2)}) copy-start(bf16[180,540]{1,0:T(8,128)(2,1)} %param.19) | copy-start | bytes 583204
  0.7 5.1 %copy-start.1 = (bf16[8,256,180]{1,0,2:T(8,128)(2,1)S(1)}, bf16[8,256,180]{1,0,2:T(8,128)(2,1)}, u32[]{:S(2)}) copy-start(bf16[8,256,180]{1,0,2:T(8,128)(2,1)} %param.12) | copy-start | bytes 2211844
  44.6 24.8 %all-to-all-start = ((bf16[8,384,128]{2,1,0:T(8,128)(2,1)}), bf16[8,384,128]{2,1,0:T(8,128)(2,1)S(1)}, u32[]{:S(2)}, u32[]{:S(2)}) async-start(bf16[8,384,128]{2,1,0:T(8,128)(2,1)} %bitcast.14), calls=%async_computation | async-start | bytes 1572864 | tf_op jit(solution)/shard_map/all_to_all | solution.py:368

commit v7 on v6

--- a/solution.py
+++ b/solution.py
@@ -185,7 +185,7 @@
 
     for c in range(chunks):
         copies[c].wait()
-        if c == chunks // 2:
+        if c == chunks // 4:
             copies[chunks].start()
         low = c * width
         block = nxt_buf[:, low : low + width].astype(F32)

time: 73.5 us -> 75 us (1.020)
  starting transfers between devices: 5.03 us -> 9.7 us
  Pallas kernels: 57.5 us -> 54.4 us
    all_to_all x1, starting transfers between devices: 5.03 us -> 9.7 us  [shards(): lax.all_to_all(outgoing.reshape(bands, -1, LANES), 'band', split_axis=0,...]
    pallas_call x1, Pallas kernels: 33.8 us -> 30.6 us  [shards(): pl.pallas_call(own_kernel, out_shape=(jax.ShapeDtypeStruct((windows, HALF...]
  transfers between devices with their start and end apart: 1 -> 1, of which waited for: 0 -> 0; matrix products, arithmetic and copies ran while one was open for 3% -> 3% of each run, Pallas kernels for 24% -> 23%
where the time goes in v7:
time: 75 us; the launch traced here: 74.6 us
  Pallas kernels  54.4 us (73%)
  starting transfers between devices  9.7 us (13%)
  local copies, waits for them, and re-layouts  7.03 us (9%)
  between operations  1.42 us (2%)
  matrix products  1.3 us (2%)
  other arithmetic  0.81 us (1%)
    pallas_call x1, Pallas kernels, shards(): pl.pallas_call(own_kernel, out_shape=(jax.ShapeDtypeStruct((windows, HALF...  30.6 us
    pallas_call x1, Pallas kernels, shards(): pl.pallas_call(map_kernel, out_shape=jax.ShapeDtypeStruct((rows, cols, ch...  17.5 us
    all_to_all x1, starting transfers between devices, shards(): lax.all_to_all(outgoing.reshape(bands, -1, LANES), 'band', split_axis=0,...  9.7 us
    unnamed x9, local copies, waits for them, and re-layouts  4.81 us
    pallas_call x1, Pallas kernels, shards(): pl.pallas_call(pack_kernel, out_shape=jax.ShapeDtypeStruct((bands * pairs...  3.61 us
    pallas_call x1, Pallas kernels, shards(): pl.pallas_call(place_kernel, out_shape=jax.ShapeDtypeStruct((CAP, TILE *...  2.68 us
  transfers between devices with their start and end apart: 1, of which 0 were waited for; matrix products, arithmetic and copies ran while one was open for 3% of the time, Pallas kernels for 23%

profile of v7, /device:TPU:0, one launch (start us, length us, event | category | flops | bytes accessed | tf_op | source)
XLA Modules:
  0.0 74.6 jit_solution(8197413020527873393)
XLA Ops:
  0.6 0.0 copy-start
  0.6 0.0 copy-start.2
  0.7 0.0 copy-start.1
  1.4 0.7 pad_add_fusion
  2.1 0.6 pad_bitcast_fusion.told
  2.7 0.1 add_add_fusion
  2.8 0.1 add.57
  2.9 0.0 copy-done
  2.9 1.3 %convolution_bitcast_fusion = f32[6,4096]{1,0:T(8,128)S(1)} fusion(f32[225,6]{0,1:T(8,128)S(1)} %copy-done, s32[4096]{0:T(1024)S(1)} %add.57), kind=kOutput, calls=%fused_computation | convolution fusion | flops 67276800 | bytes 120088 | tf_op jit(solution)/shard_map/dot_general | solution.py:313
  4.2 0.8 %reshape.97.bias = f32[6,64,64]{2,1,0:T(8,128)} reshape(f32[6,4096]{1,0:T(8,128)S(1)} %convolution_bitcast_fusion) | data formatting | bytes 196608 | tf_op jit(solution)/shard_map/reshape | solution.py:313
  5.0 0.0 copy-done.2
  5.0 0.8 %fusion.1 = (bf16[180,180]{1,0:T(8,128)(2,1)}, bf16[180,180]{1,0:T(8,128)(2,1)}, bf16[180,180]{1,0:T(8,128)(2,1)}) fusion(bf16[180,540]{1,0:T(8,128)(2,1)S(1)} %copy-done.2), kind=kLoop, calls=%fused_computation.11 | loop fusion | bytes 388800 | tf_op jit(solution)/shard_map/slice | solution.py:328
  5.8 0.0 copy-done.1
  5.8 1.5 %copy.14.pixels = bf16[8,256,180]{2,1,0:T(8,128)(2,1)} copy(bf16[8,256,180]{1,0,2:T(8,128)(2,1)S(1)} %copy-done.1) | data formatting | bytes 1474560 | tf_op args[0]
  7.2 30.6 %own.1 = (bf16[32,32,180]{2,1,0:T(8,128)(2,1)}, bf16[32,64,128]{2,1,0:T(8,128)(2,1)}, bf16[32,64,52]{2,1,0:T(8,128)(2,1)}, bf16[4,256,180]{2,1,0:T(8,128)(2,1)}, s32[1,128]{1,0:T(1,128)}) custom-call(bf16[8,256,180]{2,1,0:T(8,128)(2,1)} %copy.14.pixels, s32[1,128]{1,0:T(1,128)} %pad_bitcast_fusion.told, f32[6,64,64]{2,1,0:T(8,128)} %reshape.97.bias, ...), custom_call_target="tpu_custom_call" | custom-call | flops 3000000000 | bytes 10000000 | tf_op jit(solution)/shard_map/own/pallas_call | solution.py:333
  37.8 3.6 %pack.1 = bf16[16,192,128]{2,1,0:T(8,128)(2,1)} custom-call(s32[32]{0:T(128)} %bitcast.18, s32[1]{0:T(128)S(6)} %copy.18.count, s32[16]{0:T(128)} %bitcast.15, s32[16]{0:T(128)} %bitcast.16, bf16[32,64,128]{2,1,0:T(8,128)(2,1)} %get-tuple-element.10.first, bf16[32,64,52]{2,1,0:T(8,128)(2,1)} %get-tuple-element.11.rest), custom_call_target="tpu_custom_call" | custom-call | tf_op jit(solution)/shard_map/pack/pallas_call | solution.py:359
  41.5 9.7 %all-to-all-start = ((bf16[8,384,128]{2,1,0:T(8,128)(2,1)}), bf16[8,384,128]{2,1,0:T(8,128)(2,1)S(1)}, u32[]{:S(2)}, u32[]{:S(2)}) async-start(bf16[8,384,128]{2,1,0:T(8,128)(2,1)} %bitcast.14), calls=%async_computation | async-start | bytes 1572864 | tf_op jit(solution)/shard_map/all_to_all | solution.py:368
  51.2 17.5 %map.1 = bf16[8,256,180]{2,1,0:T(8,128)(2,1)} custom-call(s32[32]{0:T(128)} %bitcast.19, s32[1]{0:T(128)S(6)} %copy.18.count, s32[1,128]{1,0:T(1,128)} %get-tuple-element.7.facts, bf16[8,256,180]{2,1,0:T(8,128)(2,1)} %copy.14.pixels, bf16[4,256,180]{2,1,0:T(8,128)(2,1)} %get-tuple-element.8.prv, bf16[32,32,180]{2,1,0:T(8,128)(2,1)} %get-tuple-element.9.upper, ...), custom_call_target="tpu_custom_call" | custom-call | flops 10000000000 | bytes 30000000 | tf_op jit(solution)/shard_map/map/pallas_call | solution.py:371
  68.6 2.3 %copy.16 = bf16[8,256,180]{1,0,2:T(8,128)(2,1)} copy(bf16[8,256,180]{2,1,0:T(8,128)(2,1)} %map.1) | data formatting | bytes 1474560
  70.9 0.0 all-to-all-done
  70.9 2.7 %place.1 = bf16[8,128,180]{2,1,0:T(8,128)(2,1)S(1)} custom-call(bf16[16,192,128]{2,1,0:T(8,128)(2,1)S(1)} %bitcast.13), custom_call_target="tpu_custom_call" | custom-call | tf_op jit(solution)/shard_map/place/pallas_call | solution.py:390
  73.6 1.0 %copy.17 = bf16[8,128,180]{1,0,2:T(8,128)(2,1)} copy(bf16[8,128,180]{2,1,0:T(8,128)(2,1)S(1)} %place.1) | data formatting | bytes 737280
  (1 shorter events, 0.0 us)
Async XLA Ops:
  0.6 2.2 %copy-start = (f32[225,6]{0,1:T(8,128)S(1)}, f32[225,6]{0,1:T(8,128)}, u32[]{:S(2)}) copy-start(f32[225,6]{0,1:T(8,128)} %param.17) | copy-start | bytes 16204
  0.6 4.3 %copy-start.2 = (bf16[180,540]{1,0:T(8,128)(2,1)S(1)}, bf16[180,540]{1,0:T(8,128)(2,1)}, u32[]{:S(2)}) copy-start(bf16[180,540]{1,0:T(8,128)(2,1)} %param.19) | copy-start | bytes 583204
  0.7 5.1 %copy-start.1 = (bf16[8,256,180]{1,0,2:T(8,128)(2,1)S(1)}, bf16[8,256,180]{1,0,2:T(8,128)(2,1)}, u32[]{:S(2)}) copy-start(bf16[8,256,180]{1,0,2:T(8,128)(2,1)} %param.12) | copy-start | bytes 2211844
  41.5 29.5 %all-to-all-start = ((bf16[8,384,128]{2,1,0:T(8,128)(2,1)}), bf16[8,384,128]{2,1,0:T(8,128)(2,1)S(1)}, u32[]{:S(2)}, u32[]{:S(2)}) async-start(bf16[8,384,128]{2,1,0:T(8,128)(2,1)} %bitcast.14), calls=%async_computation | async-start | bytes 1572864 | tf_op jit(solution)/shard_map/all_to_all | solution.py:368
